TPU v7x, 1024 devices: a whole 4x8x16 slice. The times are simulated.
1024 devices in a mesh: dp: 32 (over z_lo, x, core), expert: 32 (over y, z_hi).
Axes of the slice: x: 4, y: 8, z: 16 (z_hi: 4, z_lo: 4; z = z_hi * 4 + z_lo), core: 2. Of those that a mesh axis runs over, the one named last changes fastest.
Arguments:
- tokens: bfloat16 [8192, 2048], P('dp', 'expert'), may hold values from -6 to 6
- out_grad: bfloat16 [8192, 2048], P('dp', 'expert'), may hold values from -6 to 6
- expert_out: bfloat16 [8192, 2048], P('dp', 'expert'), may hold values from -0.119628906 to 0.119628906
- router_probs: float32 [8192, 32], P('dp'), may hold values from 0 to 1, as said below
- expert_index: int32 [8192, 1], P('dp'), may hold values from 0 to 31; in each aligned block of 256 rows (0 to 255, 256 to 511, ...) at most 10 rows name the same one
- in_weight: bfloat16 [32, 2, 5120, 2048], P('expert', None, 'dp'), may hold values from -0.125 to 0.125
- down_weight: bfloat16 [32, 5120, 2048], P('expert', 'dp'), may hold values from -0.078125 to 0.078125
- router_weight: bfloat16 [2048, 32], P('expert'), may hold values from -6 to 6
Outputs:
- token_grad: bfloat16 [8192, 2048], P('dp', 'expert')
- in_weight_grad: bfloat16 [32, 2, 5120, 2048], P('expert', None, 'dp')
- router_grad: float32 [2048, 32], P('expert')
Inputs may be any that keep to these rules, and one draw needn't show every extreme that they name: `expert_index`: in each aligned block of 256 tokens (one group) no expert is chosen more than 10 times, so no token is dropped. `router_probs`: each row is positive and sums to one.
All inputs are finite; a program needn't handle non-finite values.
Results may differ from a plain program's by a relative error of at most 0.0057.
Values may be sent and summed in bfloat16 or wider, within the bound.
No kernel may reach another device: no remote copies, remote signals or barrier semaphores. Data moves between devices by JAX's collectives and lax.ppermute only.
A program may use at most 64 MiB of HBM per device.

v0:
```python
from functools import partial

import jax
import jax.numpy as jnp
from jax import lax
from jax.sharding import PartitionSpec as P

aux_coef = 0.2


def from_everyone(x, axis):
    copies = jnp.broadcast_to(x, (lax.axis_size(axis), *x.shape))
    return lax.all_to_all(copies, axis, split_axis=0, concat_axis=0, tiled=True)


def over_copies(x, axis):
    return from_everyone(x, axis).sum(axis=0)


def sent_together(arrays, axis, split_dim, concat_dim, along):
    both = jnp.concatenate(arrays, axis=along)
    filled, at, outs = (
        lax.all_to_all(both, axis, split_axis=split_dim, concat_axis=concat_dim, tiled=True),
        0,
        [],
    )
    for a in arrays:
        outs.append(lax.slice_in_dim(filled, at, at + a.shape[along], axis=along))
        at += a.shape[along]
    return tuple(outs)


def side_by_side(arrays, axis, dim, along):
    ends, at = ([], 0)
    for a in arrays[:-1]:
        at += a.shape[along]
        ends.append(at)
    both = jnp.concatenate(arrays, axis=along)
    return tuple(jnp.split(lax.all_gather(both, axis, axis=dim, tiled=True), ends, axis=along))


def in_blocks(x, dim, length):
    before, after = (x.shape[:dim], x.shape[dim + 1 :])
    return jnp.moveaxis(x.reshape(*before, length, -1, *after), dim, 0)


def sent_and_summed(x, axis, dim):
    length = lax.axis_size(axis)
    parts = lax.all_to_all(in_blocks(x, dim, length), axis, 0, 0, tiled=True)
    return jnp.sum(parts, axis=0)


def slot_numbers(routes):
    width = routes.shape[1]
    same_expert = routes[:, :, None] == routes[:, None, :]
    position = jnp.arange(width, dtype=jnp.int32)
    before = position[None, :] < position[:, None]
    return jnp.sum((same_expert & before[None]).astype(jnp.int32), axis=2)


def one_hot(routes, slot_ids, experts, capacity):
    expert_hit = routes[..., None] == jnp.arange(experts, dtype=jnp.int32)
    slot_hit = slot_ids[..., None] == jnp.arange(capacity, dtype=jnp.int32)
    return (expert_hit[..., :, None] & slot_hit[..., None, :]).astype(jnp.float32)


def gelu_parts(pre_act, upstream):
    gelu_value, pullback = jax.vjp(partial(jax.nn.gelu, approximate=True), pre_act)
    return (gelu_value, pullback(upstream)[0])


def per_device(
    tokens, out_grad, expert_out, router_probs, expert_index, in_weight, down_weight, router_weight
):
    token_count, feature_width = tokens.shape
    experts = router_probs.shape[1]
    capacity = (5 * token_count + 4 * experts - 1) // (4 * experts)
    groups = lax.axis_size("dp")
    routes = expert_index[:, 0]
    slot_ids = slot_numbers(routes[None, :])[0]
    dispatch_mask = one_hot(routes, slot_ids, experts, capacity)
    chosen = jnp.sum(dispatch_mask, axis=2)
    gate = jnp.sum(router_probs * chosen, axis=1)
    gated_dy = (gate[:, None] * out_grad.astype(jnp.float32)).astype(jnp.bfloat16)
    partial_dot = jnp.sum(out_grad.astype(jnp.float32) * expert_out.astype(jnp.float32), axis=1)
    gate_dot = over_copies(partial_dot, "expert")
    mask_half = dispatch_mask.astype(jnp.bfloat16)
    send_tokens = jnp.einsum(
        "tec,tf->ecf", mask_half, tokens, preferred_element_type=jnp.float32
    ).astype(jnp.bfloat16)
    send_grads = jnp.einsum(
        "tec,tf->ecf", mask_half, gated_dy, preferred_element_type=jnp.float32
    ).astype(jnp.bfloat16)
    got_tokens, got_grads = sent_together((send_tokens, send_grads), "expert", 0, 2, 1)
    counts = over_copies(jnp.sum(chosen, axis=0), "dp")
    row_tokens, row_grads = side_by_side((got_tokens[0], got_grads[0]), "dp", 0, 1)
    gate_weight = in_weight[0, 0]
    up_weight = in_weight[0, 1]
    contract_last = (((1,), (1,)), ((), ()))
    contract_first = (((0,), (0,)), ((), ()))
    gate_pre = lax.dot_general(
        row_tokens, gate_weight, contract_last, preferred_element_type=jnp.float32
    )
    up_pre = lax.dot_general(
        row_tokens, up_weight, contract_last, preferred_element_type=jnp.float32
    )
    hidden_grad = lax.dot_general(
        row_grads, down_weight[0], contract_last, preferred_element_type=jnp.float32
    )
    gate_act, gate_back = gelu_parts(gate_pre, hidden_grad * up_pre)
    gate_grad = gate_back.astype(jnp.bfloat16)
    up_grad = (hidden_grad * gate_act).astype(jnp.bfloat16)
    up_rows = lax.slice_in_dim(up_grad, 0, capacity * lax.axis_size("dp"), axis=0)
    term = jnp.dot(gate_grad, gate_weight, preferred_element_type=jnp.float32)
    summed = sent_and_summed(
        term + jnp.dot(up_rows, up_weight, preferred_element_type=jnp.float32), "dp", 0
    )
    w_gate_grad = lax.dot_general(
        gate_grad, row_tokens, contract_first, preferred_element_type=jnp.float32
    )
    w_up_grad = lax.dot_general(
        up_grad, row_tokens, contract_first, preferred_element_type=jnp.float32
    )
    weight_grad = jnp.stack([w_gate_grad, w_up_grad]).astype(jnp.bfloat16)[None]
    prob_grad = chosen * gate_dot[:, None] + aux_coef * experts * counts[None, :] / (
        token_count * groups
    )
    logit_grad = router_probs * (
        prob_grad - jnp.sum(router_probs * prob_grad, axis=1, keepdims=True)
    )
    logit_grad = logit_grad.astype(jnp.bfloat16)
    router_part = lax.dot_general(
        tokens, logit_grad, contract_first, preferred_element_type=jnp.float32
    )
    router_term = lax.dot_general(
        logit_grad, router_weight, contract_last, preferred_element_type=jnp.float32
    )
    router_grad = over_copies(router_part, "dp")
    returned = lax.all_to_all(summed[None], "expert", split_axis=2, concat_axis=0, tiled=True)
    combined = jnp.einsum("tec,ecf->tf", dispatch_mask, returned, precision=lax.Precision.HIGHEST)
    token_grad = (combined + router_term).astype(jnp.bfloat16)
    return (token_grad, weight_grad, router_grad)


def solution(mesh):
    in_specs = (
        P("dp", "expert"),
        P("dp", "expert"),
        P("dp", "expert"),
        P("dp", None),
        P("dp", None),
        P("expert", None, "dp", None),
        P("expert", "dp", None),
        P("expert", None),
    )
    out_specs = (P("dp", "expert"), P("expert", None, "dp", None), P("expert", None))
    return jax.shard_map(
        per_device, mesh=mesh, in_specs=in_specs, out_specs=out_specs, check_vma=False
    )
```

profile of v0, /device:TPU:1, one launch (start us, length us, event | category | flops | bytes accessed | tf_op | source)
XLA Modules:
  0.0 319.2 jit_solution(8309966576126677646)
XLA Ops:
  7.2 0.9 convert_reduce_fusion.2
  9.6 17.6 %all-to-all-start.4 = ((f32[32,1,32]{2,1,0:T(1,128)}), f32[32,1,32]{2,1,0:T(1,128)S(1)}, u32[]{:S(2)}, u32[]{:S(2)}) async-start(f32[32,1,32]{2,1,0:T(1,128)} %broadcast_in_dim.10), calls=%async_computation.4 | async-start | bytes 32768 | tf_op jit(solution)/shard_map/all_to_all | solution.py:13
  27.2 0.9 convolution_convert_fusion.3
  28.2 0.8 fusion.41
  29.0 5.6 %all-to-all-done.4 = f32[32,1,32]{2,1,0:T(1,128)S(1)} async-done(((f32[32,1,32]{2,1,0:T(1,128)}), f32[32,1,32]{2,1,0:T(1,128)S(1)}, u32[]{:S(2)}, u32[]{:S(2)}) %all-to-all-start.4) | async-done | bytes 4128 | tf_op jit(solution)/shard_map/all_to_all | solution.py:13
  35.2 15.1 %all-to-all-start.3 = ((f32[32,1,256]{2,1,0:T(1,128)}), f32[32,1,256]{2,1,0:T(1,128)S(1)}, u32[]{:S(2)}, u32[]{:S(2)}) async-start(f32[32,1,256]{2,1,0:T(1,128)} %broadcast_in_dim.9), calls=%async_computation.3 | async-start | bytes 65536 | tf_op jit(solution)/shard_map/all_to_all | solution.py:13
  50.4 15.8 %all-to-all-done.3 = f32[32,1,256]{2,1,0:T(1,128)S(1)} async-done(((f32[32,1,256]{2,1,0:T(1,128)}), f32[32,1,256]{2,1,0:T(1,128)S(1)}, u32[]{:S(2)}, u32[]{:S(2)}) %all-to-all-start.3) | async-done | bytes 32800 | tf_op jit(solution)/shard_map/all_to_all | solution.py:13
  66.2 0.8 multiply_reduce_fusion
  67.1 0.9 convolution_convert_fusion.2
  68.3 19.0 %all_to_all.58 = bf16[32,2,640]{2,1,0:T(2,128)(2,1)S(1)} all-to-all(bf16[32,2,640]{2,1,0:T(2,128)(2,1)S(1)} %reshape.191), channel_id=1, replica_groups=mesh['dp'=32,'expert'=32] {'expert'}, dimensions={0} | all-to-all | bytes 163840 | tf_op jit(solution)/shard_map/all_to_all | solution.py:23
  88.7 1.0 reshape.195
  89.7 6.7 %all-to-all-start.5 = ((f32[32,1,2048]{2,1,0:T(1,128)}), f32[32,1,2048]{2,1,0:T(1,128)S(1)}, u32[]{:S(2)}, u32[]{:S(2)}) async-start(f32[32,1,2048]{2,1,0:T(1,128)} %reshape.195), calls=%async_computation.5 | async-start | bytes 524288 | tf_op jit(solution)/shard_map/all_to_all | solution.py:13
  96.4 54.4 %all-gather.3.cloned.1.call-done = bf16[32,10,4096]{2,1,0:T(8,128)(2,1)} async-done(((bf16[1,10,4096]{2,1,0:T(8,128)(2,1)}), bf16[32,10,4096]{2,1,0:T(8,128)(2,1)}) %all-gather.3.cloned.1.call-update) | async-done | bytes 2621456 | tf_op jit(solution)/shard_map/all_gather | solution.py:39
  150.8 3.3 %reshape.187 = bf16[320,4096]{1,0:T(8,128)(2,1)S(1)} reshape(bf16[32,10,4096]{2,1,0:T(8,128)(2,1)} %all-gather.3.cloned.1.call-done) | data formatting | bytes 5242880
  154.1 2.2 fusion.7
  159.6 2.2 reshape.185
  162.5 5.0 %all-to-all-start.1 = ((f32[32,10,2048]{2,1,0:T(8,128)}), f32[32,10,2048]{2,1,0:T(8,128)}, u32[]{:S(2)}, u32[]{:S(2)}) async-start(f32[32,10,2048]{2,1,0:T(8,128)} %reshape.185), calls=%async_computation.1 | async-start | bytes 8388608 | tf_op jit(solution)/shard_map/all_to_all | solution.py:49
  168.0 2.2 reduce.6
  170.3 1.0 reshape.196
  171.3 1.7 bitcast_reduce_fusion
  173.0 2.3 fusion
  175.3 85.3 %all-to-all-done.1 = f32[32,10,2048]{2,1,0:T(8,128)} async-done(((f32[32,10,2048]{2,1,0:T(8,128)}), f32[32,10,2048]{2,1,0:T(8,128)}, u32[]{:S(2)}, u32[]{:S(2)}) %all-to-all-start.1) | async-done | bytes 2621472 | tf_op jit(solution)/shard_map/all_to_all | solution.py:49
  260.6 2.4 reduce_sum.93
  263.0 1.9 copy.34
  264.9 11.4 %reduce.4 = f32[2048,10]{1,0:T(8,128)} reduce(f32[2048,1,10]{2,1,0:T(1,128)} %bitcast.65, f32[]{:T(128)} %broadcast.109), dimensions={1}, to_apply=%bitcast.49.reduce_sub_computation | reduce | bytes 163844
  276.3 2.6 reshape.193
  278.9 13.2 %all-to-all-start.2 = ((f32[32,1,640]{2,1,0:T(1,128)}), f32[32,1,640]{2,1,0:T(1,128)S(1)}, u32[]{:S(2)}, u32[]{:S(2)}) async-start(f32[32,1,640]{2,1,0:T(1,128)} %reshape.193), calls=%async_computation.2 | async-start | bytes 163840 | tf_op jit(solution)/shard_map/all_to_all | solution.py:139
  293.3 1.2 pad_maximum_fusion
  294.5 13.8 %all-to-all-done.2 = f32[32,1,640]{2,1,0:T(1,128)S(1)} async-done(((f32[32,1,640]{2,1,0:T(1,128)}), f32[32,1,640]{2,1,0:T(1,128)S(1)}, u32[]{:S(2)}, u32[]{:S(2)}) %all-to-all-start.2) | async-done | bytes 81952 | tf_op jit(solution)/shard_map/all_to_all | solution.py:139
  308.3 0.8 reduce.5
  309.1 1.7 reshape.194
  311.5 0.8 fusion.4
  (62 shorter events, 10.0 us)
Async XLA Ops:
  7.2 149.2 %copy-start = (bf16[1,160,2048]{2,1,0:T(8,128)(2,1)S(1)}, bf16[1,160,2048]{2,1,0:T(8,128)(2,1)}, u32[]{:S(2)}) copy-start(bf16[1,160,2048]{2,1,0:T(8,128)(2,1)} %param.14) | copy-start | bytes 1966084
  8.8 59.3 %copy-start.10 = (pred[256,32]{0,1:T(8,128)(4,1)}, pred[256,32]{0,1:T(8,128)(4,1)S(1)}, u32[]{:S(2)}) copy-start(pred[256,32]{0,1:T(8,128)(4,1)S(1)} %iota_compare_fusion.1) | copy-start | bytes 24580
  8.8 59.3 %copy-start.12 = (pred[256,10]{0,1:T(8,128)(4,1)}, pred[256,10]{0,1:T(8,128)(4,1)S(1)}, u32[]{:S(2)}) copy-start(pred[256,10]{0,1:T(8,128)(4,1)S(1)} %iota_compare_fusion.2) | copy-start | bytes 7684
  9.6 25.0 %all-to-all-start.4 = ((f32[32,1,32]{2,1,0:T(1,128)}), f32[32,1,32]{2,1,0:T(1,128)S(1)}, u32[]{:S(2)}, u32[]{:S(2)}) async-start(f32[32,1,32]{2,1,0:T(1,128)} %broadcast_in_dim.10), calls=%async_computation.4 | async-start | bytes 32768 | tf_op jit(solution)/shard_map/all_to_all | solution.py:13
  35.2 30.9 %all-to-all-start.3 = ((f32[32,1,256]{2,1,0:T(1,128)}), f32[32,1,256]{2,1,0:T(1,128)S(1)}, u32[]{:S(2)}, u32[]{:S(2)}) async-start(f32[32,1,256]{2,1,0:T(1,128)} %broadcast_in_dim.9), calls=%async_computation.3 | async-start | bytes 65536 | tf_op jit(solution)/shard_map/all_to_all | solution.py:13
  50.3 100.5 %all-gather.3.cloned.1.call-start = ((), (), s32[]{:S(2)}) async-start(), calls=%async_computation.6 | async-start | bytes 4325376 | tf_op jit(solution)/shard_map/all_gather | solution.py:39
  68.0 20.4 %copy-start.9 = (f32[256,32]{0,1:T(8,128)S(1)}, f32[256,32]{0,1:T(8,128)}, u32[]{:S(2)}) copy-start(f32[256,32]{0,1:T(8,128)} %param.11) | copy-start | bytes 98308
  68.0 20.4 %copy-start.14 = (bf16[256,64]{0,1:T(8,128)(2,1)S(1)}, bf16[256,64]{0,1:T(8,128)(2,1)}, u32[]{:S(2)}) copy-start(bf16[256,64]{0,1:T(8,128)(2,1)} %param.8) | copy-start | bytes 98308
  89.7 72.1 %all-to-all-start.5 = ((f32[32,1,2048]{2,1,0:T(1,128)}), f32[32,1,2048]{2,1,0:T(1,128)S(1)}, u32[]{:S(2)}, u32[]{:S(2)}) async-start(f32[32,1,2048]{2,1,0:T(1,128)} %reshape.195), calls=%async_computation.5 | async-start | bytes 524288 | tf_op jit(solution)/shard_map/all_to_all | solution.py:13
  154.1 2.9 copy-start.1
  156.4 1.3 copy-start.4
  157.0 2.0 copy-start.6
  158.4 0.6 copy-start.8
  161.8 0.7 copy-start.5
  161.8 11.2 %copy-start.2 = (bf16[320,4096]{1,0:T(8,128)(2,1)S(1)}, bf16[320,4096]{1,0:T(8,128)(2,1)}, u32[]{:S(2)}) copy-start(bf16[320,4096]{1,0:T(8,128)(2,1)} %copy-done.1) | copy-start | bytes 7864324
  162.5 98.1 %all-to-all-start.1 = ((f32[32,10,2048]{2,1,0:T(8,128)}), f32[32,10,2048]{2,1,0:T(8,128)}, u32[]{:S(2)}, u32[]{:S(2)}) async-start(f32[32,10,2048]{2,1,0:T(8,128)} %reshape.185), calls=%async_computation.1 | async-start | bytes 8388608 | tf_op jit(solution)/shard_map/all_to_all | solution.py:49
  264.9 27.3 %copy-start.7 = (bf16[320,160]{0,1:T(8,128)(2,1)S(1)}, bf16[320,160]{0,1:T(8,128)(2,1)}, u32[]{:S(2)}) copy-start(bf16[320,160]{0,1:T(8,128)(2,1)} %copy-done.6) | copy-start | bytes 307204
  278.9 29.3 %all-to-all-start.2 = ((f32[32,1,640]{2,1,0:T(1,128)}), f32[32,1,640]{2,1,0:T(1,128)S(1)}, u32[]{:S(2)}, u32[]{:S(2)}) async-start(f32[32,1,640]{2,1,0:T(1,128)} %reshape.193), calls=%async_computation.2 | async-start | bytes 163840 | tf_op jit(solution)/shard_map/all_to_all | solution.py:139
  292.2 1.1 copy-start.3
  294.5 16.7 %copy-start.11 = (pred[256,32]{0,1:T(8,128)(4,1)S(1)}, pred[256,32]{0,1:T(8,128)(4,1)}, u32[]{:S(2)}) copy-start(pred[256,32]{0,1:T(8,128)(4,1)} %copy-done.10) | copy-start | bytes 24580
  294.5 16.7 %copy-start.13 = (pred[256,10]{0,1:T(8,128)(4,1)S(1)}, pred[256,10]{0,1:T(8,128)(4,1)}, u32[]{:S(2)}) copy-start(pred[256,10]{0,1:T(8,128)(4,1)} %copy-done.12) | copy-start | bytes 7684
  309.1 2.4 copy-start.15
Sparse Core Ops, SparseCore 0:
  88.5 62.2 all-gather.2
where the time goes:
time: 321 us; the launch traced here: 319 us
  waiting for transfers between devices  175 us (55%)
  starting transfers between devices  57.7 us (18%)
  other arithmetic  24.1 us (8%)
  blocking collectives  19 us (6%)
  local copies, waits for them, and re-layouts  18.6 us (6%)
  between operations  14.4 us (4%)
  matrix products  10.6 us (3%)
    all_to_all x1, waiting for transfers between devices, sent_and_summed(): parts = lax.all_to_all(in_blocks(x, dim, length), axis, 0, 0, tiled=True)  85.3 us
    all_gather x1, waiting for transfers between devices, side_by_side(): lax.all_gather(both, axis, axis=dim, tiled=True)  54.4 us
    all_to_all x3, starting transfers between devices, from_everyone(): return lax.all_to_all(copies, axis, split_axis=0, concat_axis=0, tiled=True)  39.4 us
    all_to_all x3, waiting for transfers between devices, from_everyone(): return lax.all_to_all(copies, axis, split_axis=0, concat_axis=0, tiled=True)  21.4 us
    all_to_all x1, blocking collectives, sent_together(): lax.all_to_all(both, axis, split_axis=split_dim, concat_axis=concat_dim,...  19 us
    all_to_all x1, waiting for transfers between devices, per_device(): lax.all_to_all(summed[None], 'expert', split_axis=2, concat_axis=0, tiled...  13.8 us
    all_to_all x1, starting transfers between devices, per_device(): lax.all_to_all(summed[None], 'expert', split_axis=2, concat_axis=0, tiled...  13.2 us
    unnamed x41, local copies, waits for them, and re-layouts  12.6 us
  transfers between devices with their start and end apart: 6, of which 5 were waited for; matrix products, arithmetic and copies ran while one was open for 7% of the time, Pallas kernels for 0%

commit v1 on v0

v1 whole, which is shorter than its diff:
```python
import jax
import jax.numpy as jnp
from jax import lax
from jax.experimental import pallas as pl
from jax.experimental.pallas import tpu as pltpu
from jax.sharding import Mesh, PartitionSpec as P

ZL, X, CORE, Y, ZH = 4, 4, 2, 8, 4
EX = ("y", "zh")
DP = ("zl", "x", "core")
E = 32
CAP = 10
T = 256
F = 64
D = 2048
KT = 2 * D // 128
AUX = 0.2
F32, BF16 = jnp.float32, jnp.bfloat16
CONTRACT_LAST = (((1,), (1,)), ((), ()))
CONTRACT_FIRST = (((0,), (0,)), ((), ()))


def vmem(n):
    return [pl.BlockSpec(memory_space=pltpu.VMEM)] * n


def iota(shape, dim):
    return lax.broadcasted_iota(jnp.int32, shape, dim)


def slots(idx):
    hit = iota((E, T), 0) == idx
    hot = jnp.where(hit, 1.0, 0.0).astype(F32)
    earlier = jnp.where(iota((T, T), 0) < iota((T, T), 1), 1.0, 0.0).astype(BF16)
    before = jnp.dot(hot.astype(BF16), earlier, preferred_element_type=F32)
    return hot, jnp.sum(hot * before, axis=0, keepdims=True)


def dispatch_kernel(tok, og, eo, probs, idx_ref, out):
    idx = idx_ref[...]
    hot, slot = slots(idx)
    gate = jnp.sum(probs[...] * hot, axis=0, keepdims=True)
    grad = og[...].astype(F32)
    gated = (gate * grad).astype(BF16)
    dot = jnp.sum(grad * eo[...].astype(F32), axis=0, keepdims=True)
    row = iota((E * 16, T), 0)
    sel = jnp.where(
        (lax.shift_right_logical(row, 4) == idx) & (lax.bitwise_and(row, 15) == slot.astype(jnp.int32)),
        1.0,
        0.0,
    ).astype(BF16)
    both = jnp.concatenate([tok[...], gated], axis=0)
    sent = lax.dot_general(sel, both, CONTRACT_LAST, preferred_element_type=F32)
    h0 = dot.astype(BF16).astype(F32)
    h1 = (dot - h0).astype(BF16).astype(F32)
    h2 = dot - h0 - h1
    line = iota((16, 128), 0)
    extra = jnp.zeros((16, 128), F32)
    for i, h in enumerate((h0, h1, h2)):
        for j in range(2):
            extra = extra + jnp.where(line == CAP + 2 * i + j, h[:, 128 * j : 128 * (j + 1)], 0.0)
    out[...] = (sent.reshape(E, 16, 128) + extra[None]).astype(BF16)


def pack_kernel(got, idx_ref, out, dot_ref):
    lane = iota((16, 128), 1)
    low = lane < F
    tail = [jnp.zeros((8, 128), F32) for _ in range(KT // 4)]
    line = iota((8, 128), 0)
    total = jnp.zeros((16, 128), F32)
    for j in range(E // 2):
        a = got[2 * j].astype(F32)
        b = got[2 * j + 1].astype(F32)
        total = total + a + b
        t = jnp.where(low, a, pltpu.roll(b, F, 1))
        g = jnp.where(low, pltpu.roll(a, F, 1), b)
        for k, v in ((j, t), (j + E // 2, g)):
            head = v[:8].astype(BF16)
            for z in range(ZL):
                out[z, k] = head
            i = k % 4
            rest = v[8:] if i == 0 else pltpu.roll(v[8:], 2 * i, 0)
            tail[k // 4] = jnp.where((line >= 2 * i) & (line < 2 * i + 2), rest, tail[k // 4])
    for m in range(KT // 4):
        for z in range(ZL):
            out[z, KT + m] = tail[m].astype(BF16)
    hot = jnp.where(iota((128, T), 0) == idx_ref[...], 1.0, 0.0).astype(BF16)
    counts = lax.dot_general(jnp.ones((8, T), BF16), hot, CONTRACT_LAST, preferred_element_type=F32)
    for z in range(ZL):
        out[z, KT + KT // 4] = counts.astype(BF16)
    pick = jnp.where((line >= 2) & (lax.bitwise_and(line, 1) == 0), 1.0, 0.0)
    pick1 = jnp.where((line >= 2) & (lax.bitwise_and(line, 1) == 1), 1.0, 0.0)
    dot_ref[:, :128] = jnp.sum(total[8:] * pick, axis=0, keepdims=True)
    dot_ref[:, 128:] = jnp.sum(total[8:] * pick1, axis=0, keepdims=True)


def combine_kernel(ret, idx_ref, lg, rw, out):
    idx = idx_ref[...]
    _, slot = slots(idx)
    slot = slot.astype(jnp.int32)
    row = iota((E * 8, T), 0)
    mine = lax.shift_right_logical(row, 3) == idx
    c = lax.bitwise_and(row, 7)
    r = ret[...].reshape(E * 8, 128)
    acc = lax.dot_general(rw[...], lg[...], CONTRACT_FIRST, preferred_element_type=F32)
    for h in range(2):
        sel = jnp.where(mine & (c < 5) & (c + 5 * h == slot), 1.0, 0.0).astype(BF16)
        p = lax.dot_general(r, sel, CONTRACT_FIRST, preferred_element_type=F32)
        acc = acc + p[F * h : F * (h + 1)]
    out[...] = acc.astype(BF16)


def rows_of(got):
    n = got.shape[0]
    head = got[:, :KT].transpose(0, 2, 1, 3).reshape(n * 8, 2 * D)
    tail = got[:, KT : KT + KT // 4].reshape(n, KT // 4, 4, 2, 128)
    tail = tail.transpose(0, 3, 1, 2, 4).reshape(n * 2, 2 * D)
    return jnp.concatenate([head, tail], axis=0)


def backward(rows, in_w, down_w):
    tok, dy = rows[:, :D], rows[:, D:]
    gate_pre = lax.dot_general(tok, in_w[0], CONTRACT_LAST, preferred_element_type=F32)
    up_pre = lax.dot_general(tok, in_w[1], CONTRACT_LAST, preferred_element_type=F32)
    hidden = lax.dot_general(dy, down_w, CONTRACT_LAST, preferred_element_type=F32)
    act, pull = jax.vjp(lambda v: jax.nn.gelu(v, approximate=True), gate_pre)
    gate_grad = pull(hidden * up_pre)[0].astype(BF16)
    up_grad = (hidden * act).astype(BF16)
    return gate_grad, up_grad


def per_device(tokens, out_grad, expert_out, probs, idx, in_weight, down_weight, router_weight):
    tok, og, eo, pt, ix = tokens.T, out_grad.T, expert_out.T, probs.T, idx.T
    in_w, down_w = in_weight[0], down_weight[0]
    send = pl.pallas_call(
        dispatch_kernel,
        out_shape=jax.ShapeDtypeStruct((E, 16, 128), BF16),
        in_specs=vmem(5),
        out_specs=vmem(1)[0],
        name="dispatch",
    )(tok, og, eo, pt, ix)
    got = lax.all_to_all(send, EX, 0, 0, tiled=True)
    packed, gate_dot = pl.pallas_call(
        pack_kernel,
        out_shape=(
            jax.ShapeDtypeStruct((ZL, KT + KT // 4 + 1, 8, 128), BF16),
            jax.ShapeDtypeStruct((1, T), F32),
        ),
        in_specs=vmem(2),
        out_specs=tuple(vmem(2)),
        name="pack",
    )(got, ix)
    line = lax.all_to_all(packed, "zl", 0, 0, tiled=True)
    plane = lax.all_to_all(jnp.broadcast_to(line, (X, *line.shape)), "x", 0, 0, tiled=True)
    own = plane.reshape(X * ZL, *line.shape[1:])
    other = lax.ppermute(own, "core", [(0, 1), (1, 0)])

    counts = jnp.sum(own[:, -1, 0, :E].astype(F32), axis=0) + jnp.sum(
        other[:, -1, 0, :E].astype(F32), axis=0
    )
    hot = (jnp.arange(E, dtype=jnp.int32)[:, None] == ix).astype(F32)
    prob_grad = hot * gate_dot + (AUX * E * counts / (T * E))[:, None]
    lg = (pt * (prob_grad - jnp.sum(pt * prob_grad, axis=0, keepdims=True))).astype(BF16)
    router_part = lax.dot_general(lg, tok, CONTRACT_LAST, preferred_element_type=F32)
    copies = jnp.broadcast_to(router_part.reshape(1, 1, E * F), (E, 1, E * F))
    router_sum = jnp.sum(lax.all_to_all(copies, DP, 0, 0, tiled=True), axis=(0, 1)).reshape(E, F)

    own_rows, other_rows = rows_of(own), rows_of(other)
    gg_o, ug_o = backward(other_rows, in_w, down_w)
    gg_m, ug_m = backward(own_rows, in_w, down_w)

    def row_grad(gg, ug):
        return jnp.dot(gg, in_w[0], preferred_element_type=F32) + jnp.dot(
            ug, in_w[1], preferred_element_type=F32
        )

    from_core = lax.ppermute(row_grad(gg_o, ug_o).astype(BF16), "core", [(0, 1), (1, 0)])
    mine = row_grad(gg_m, ug_m) + from_core.astype(F32)
    half = mine.astype(BF16)
    n = X * ZL
    to_x = jnp.concatenate(
        [half[: 8 * n].reshape(X, 8 * ZL, D), half[8 * n :].reshape(X, 2 * ZL, D)], axis=1
    )
    part = jnp.sum(lax.all_to_all(to_x, "x", 0, 0, tiled=True).astype(F32), axis=0).astype(BF16)
    to_z = jnp.concatenate(
        [part[: 8 * ZL].reshape(ZL, 8, D), part[8 * ZL :].reshape(ZL, 2, D)], axis=1
    )
    done = jnp.sum(lax.all_to_all(to_z, "zl", 0, 0, tiled=True).astype(F32), axis=0).astype(BF16)
    back = done.reshape(2, 5, E, F).transpose(2, 1, 0, 3).reshape(E, 5, 128)
    back = jnp.pad(back, ((0, 0), (0, 3), (0, 0)))
    ret = lax.all_to_all(back, EX, 0, 0, tiled=True)

    def weight_grad(a, b):
        return lax.dot_general(a, own_rows[:, :D], CONTRACT_FIRST, preferred_element_type=F32) + (
            lax.dot_general(b, other_rows[:, :D], CONTRACT_FIRST, preferred_element_type=F32)
        )

    weights = jnp.stack([weight_grad(gg_m, gg_o), weight_grad(ug_m, ug_o)]).astype(BF16)[None]
    token_grad = pl.pallas_call(
        combine_kernel,
        out_shape=jax.ShapeDtypeStruct((F, T), BF16),
        in_specs=vmem(4),
        out_specs=vmem(1)[0],
        name="combine",
    )(ret, ix, lg, router_weight.T)
    return token_grad.T, weights, router_sum.T


def solution(mesh):
    fine = Mesh(mesh.devices.reshape(ZL, X, CORE, Y, ZH), DP + EX)
    in_specs = (
        P(DP, EX),
        P(DP, EX),
        P(DP, EX),
        P(DP, None),
        P(DP, None),
        P(EX, None, DP, None),
        P(EX, DP, None),
        P(EX, None),
    )
    out_specs = (P(DP, EX), P(EX, None, DP, None), P(EX, None))
    return jax.shard_map(
        per_device, mesh=fine, in_specs=in_specs, out_specs=out_specs, check_vma=False
    )
```

time: 321 us -> 170 us (0.53)
  waiting for transfers between devices: 175 us -> 39.4 us
  blocking collectives: 19 us -> 71 us
  starting transfers between devices: 57.7 us -> 30.3 us
  other arithmetic: 24.1 us -> 4.97 us
  between operations: 14.4 us -> 1.07 us
  local copies, waits for them, and re-layouts: 18.6 us -> 11.2 us
  Pallas kernels: 0 us -> 5.59 us
  matrix products: 10.6 us -> 5.7 us
    all_to_all x5 -> x4, waiting for transfers between devices: 121 us -> 38.4 us  [the longest x1 13.9 us: per_device(): ret = lax.all_to_all(back, EX, 0, 0, tiled=True)]
    all_gather x1 -> x0, waiting for transfers between devices: 54.4 us -> none  [side_by_side(): lax.all_gather(both, axis, axis=dim, tiled=True)]
    all_to_all x1 -> x3, blocking collectives: 19 us -> 71 us  [the longest x1 41.1 us: per_device(): got = lax.all_to_all(send, EX, 0, 0, tiled=True)]
    all_to_all x5 -> x4, starting transfers between devices: 57.6 us -> 20.9 us  [the longest x1 7 us: per_device(): ret = lax.all_to_all(back, EX, 0, 0, tiled=True)]
    unnamed x2 -> x0, other arithmetic: 12.1 us -> none
    ppermute x0 -> x2, starting transfers between devices: none -> 9.47 us  [the longest x1 7.42 us: per_device(): other = lax.ppermute(own, 'core', [(0, 1), (1, 0)])]
    unnamed x41 -> x35, local copies, waits for them, and re-layouts: 12.6 us -> 4.41 us
    pallas_call x0 -> x3, Pallas kernels: none -> 5.59 us  [the longest x1 1.92 us: per_device(): pl.pallas_call(dispatch_kernel, out_shape=jax.ShapeDtypeStruct((E, 16, 12...]
where the time goes in v1:
time: 170 us; the launch traced here: 169 us
  blocking collectives  71 us (42%)
  waiting for transfers between devices  39.4 us (23%)
  starting transfers between devices  30.3 us (18%)
  local copies, waits for them, and re-layouts  11.2 us (7%)
  matrix products  5.7 us (3%)
  Pallas kernels  5.59 us (3%)
  other arithmetic  4.97 us (3%)
    all_to_all x1, blocking collectives, per_device(): got = lax.all_to_all(send, EX, 0, 0, tiled=True)  41.1 us
    all_to_all x1, blocking collectives, per_device(): lax.all_to_all(jnp.broadcast_to(line, (X, *line.shape)), 'x', 0, 0, tiled...  17.5 us
    all_to_all x1, waiting for transfers between devices, per_device(): ret = lax.all_to_all(back, EX, 0, 0, tiled=True)  13.9 us
    all_to_all x1, blocking collectives, per_device(): line = lax.all_to_all(packed, 'zl', 0, 0, tiled=True)  12.3 us
    all_to_all x1, waiting for transfers between devices, per_device(): lax.all_to_all(to_x, 'x', 0, 0, tiled=True).astype(F32)  9.15 us
    all_to_all x1, waiting for transfers between devices, per_device(): lax.all_to_all(copies, DP, 0, 0, tiled=True)  8.19 us
    ppermute x1, starting transfers between devices, per_device(): other = lax.ppermute(own, 'core', [(0, 1), (1, 0)])  7.42 us
    all_to_all x1, waiting for transfers between devices, per_device(): lax.all_to_all(to_z, 'zl', 0, 0, tiled=True).astype(F32)  7.18 us
  transfers between devices with their start and end apart: 6, of which 5 were waited for; matrix products, arithmetic and copies ran while one was open for 7% of the time, Pallas kernels for 0%

profile of v1, /device:TPU:1, one launch (start us, length us, event | category | flops | bytes accessed | tf_op | source)
XLA Modules:
  0.0 169.3 jit_solution(10912511830454630477)
XLA Ops:
  0.6 1.9 %dispatch.1 = bf16[32,16,128]{2,1,0:T(8,128)(2,1)} custom-call(bf16[64,256]{1,0:T(8,128)(2,1)} %bitcast.96, bf16[64,256]{1,0:T(8,128)(2,1)} %bitcast.98, bf16[64,256]{1,0:T(8,128)(2,1)} %bitcast.99, f32[32,256]{1,0:T(8,128)} %bitcast.95, s32[1,256]{1,0:T(1,128)} %bitcast.100), custom_call_target="tpu_custom_call" | custom-call | tf_op jit(solution)/shard_map/dispatch/pallas_call | solution.py:135
  2.6 41.1 %all_to_all.35.got = bf16[32,16,128]{2,1,0:T(8,128)(2,1)} all-to-all(bf16[32,16,128]{2,1,0:T(8,128)(2,1)} %dispatch.1), channel_id=1, replica_groups=mesh['zl'=4,'x'=4,'core'=2,'y'=8,'zh'=4] {'y','zh'}, dimensions={0} | all-to-all | bytes 262144 | tf_op jit(solution)/shard_map/all_to_all | solution.py:142
  43.7 1.8 %pack.1 = (bf16[4,41,8,128]{3,2,1,0:T(8,128)(2,1)}, f32[1,256]{1,0:T(1,128)}) custom-call(bf16[32,16,128]{2,1,0:T(8,128)(2,1)} %all_to_all.35.got, s32[1,256]{1,0:T(1,128)} %bitcast.101), custom_call_target="tpu_custom_call" | custom-call | tf_op jit(solution)/shard_map/pack/pallas_call | solution.py:143
  45.5 12.3 %all_to_all.36 = bf16[4,41,8,128]{3,2,1,0:T(8,128)(2,1)S(1)} all-to-all(bf16[4,41,8,128]{3,2,1,0:T(8,128)(2,1)} %get-tuple-element.5), channel_id=1, replica_groups=mesh['zl'=4,'x'=4,'core'=2,'y'=8,'zh'=4] {'zl'}, dimensions={0} | all-to-all | bytes 671744 | tf_op jit(solution)/shard_map/all_to_all | solution.py:153
  58.0 17.5 %all_to_all.37 = bf16[4,4,41,8,128]{4,3,2,1,0:T(8,128)(2,1)S(1)} all-to-all(bf16[4,4,41,8,128]{4,3,2,1,0:T(8,128)(2,1)S(1)} %broadcast_in_dim.6), channel_id=1, replica_groups=mesh['zl'=4,'x'=4,'core'=2,'y'=8,'zh'=4] {'x'}, dimensions={0} | all-to-all | bytes 2686976 | tf_op jit(solution)/shard_map/all_to_all | solution.py:154
  75.9 1.2 slice_bitcast_fusion.1
  77.3 7.4 %collective-permute-start = (bf16[16,41,8,128]{3,2,1,0:T(8,128)(2,1)S(1)}, bf16[16,41,8,128]{3,2,1,0:T(8,128)(2,1)}, u32[]{:S(2)}, u32[]{:S(2)}) collective-permute-start(bf16[16,41,8,128]{3,2,1,0:T(8,128)(2,1)S(1)} %bitcast.87), channel_id=1, source_target_pairs={{0,32},{32,0},{1,33},{33,1},{2,34},{34,2},{3,35},{35,3},{4,36},{36... | collective-permute-start | bytes 4030472 | tf_op jit(solution)/shard_map/ppermute | solution.py:156
  84.9 0.9 reshape.102
  85.8 1.7 %bitcast_dynamic-update-slice_fusion = bf16[160,4096]{1,0:T(8,128)(2,1)S(1)} fusion(bf16[16,8,32,128]{3,2,1,0:T(8,128)(2,1)} %slice_bitcast_fusion.1), kind=kLoop, calls=%fused_computation.15 | loop fusion | bytes 2097152
  87.6 1.1 fusion.16
  88.7 1.0 slice.81
  90.0 1.3 slice_bitcast_fusion
  93.2 2.1 %collective-permute-start.1 = (bf16[160,2048]{1,0:T(8,128)(2,1)S(1)}, bf16[160,2048]{1,0:T(8,128)(2,1)S(1)}, u32[]{:S(2)}, u32[]{:S(2)}) collective-permute-start(bf16[160,2048]{1,0:T(8,128)(2,1)S(1)} %fusion), channel_id=1, source_target_pairs={{0,32},{32,0},{1,33},{33,1},{2,34},{34,2},{3,35},{35,3},{4,36},{36... | collective-permute-start | bytes 1966088 | tf_op jit(solution)/shard_map/ppermute | solution.py:177
  96.4 1.0 collective-permute-done.1
  97.7 0.9 pad_maximum_fusion.2
  98.6 3.5 %all-to-all-start.3 = ((bf16[4,40,2048]{2,1,0:T(8,128)(2,1)}), bf16[4,40,2048]{2,1,0:T(8,128)(2,1)S(1)}, u32[]{:S(2)}, u32[]{:S(2)}) async-start(bf16[4,40,2048]{2,1,0:T(8,128)(2,1)} %pad_maximum_fusion.2), calls=%async_computation.3 | async-start | bytes 1310720 | tf_op jit(solution)/shard_map/all_to_all | solution.py:184
  102.2 0.8 fusion.61
  103.0 0.8 fusion.60
  103.8 9.2 %all-to-all-done.3 = bf16[4,40,2048]{2,1,0:T(8,128)(2,1)S(1)} async-done(((bf16[4,40,2048]{2,1,0:T(8,128)(2,1)}), bf16[4,40,2048]{2,1,0:T(8,128)(2,1)S(1)}, u32[]{:S(2)}, u32[]{:S(2)}) %all-to-all-start.3) | async-done | bytes 655392 | tf_op jit(solution)/shard_map/all_to_all | solution.py:184
  113.1 0.7 pad_maximum_fusion.3
  113.9 4.6 %all-to-all-start.4 = ((bf16[4,10,2048]{2,1,0:T(8,128)(2,1)}), bf16[4,10,2048]{2,1,0:T(8,128)(2,1)S(1)}, u32[]{:S(2)}, u32[]{:S(2)}) async-start(bf16[4,10,2048]{2,1,0:T(8,128)(2,1)} %pad_maximum_fusion.3), calls=%async_computation.4 | async-start | bytes 524288 | tf_op jit(solution)/shard_map/all_to_all | solution.py:188
  118.9 7.2 %all-to-all-done.4 = bf16[4,10,2048]{2,1,0:T(8,128)(2,1)S(1)} async-done(((bf16[4,10,2048]{2,1,0:T(8,128)(2,1)}), bf16[4,10,2048]{2,1,0:T(8,128)(2,1)S(1)}, u32[]{:S(2)}, u32[]{:S(2)}) %all-to-all-start.4) | async-done | bytes 163872 | tf_op jit(solution)/shard_map/all_to_all | solution.py:188
  126.0 0.8 broadcast_in_dim.16
  126.9 5.8 %all-to-all-start.6 = ((f32[32,1,2048]{2,1,0:T(1,128)}), f32[32,1,2048]{2,1,0:T(1,128)S(1)}, u32[]{:S(2)}, u32[]{:S(2)}) async-start(f32[32,1,2048]{2,1,0:T(1,128)} %broadcast_in_dim.16), calls=%async_computation.6 | async-start | bytes 524288 | tf_op jit(solution)/shard_map/all_to_all | solution.py:166
  135.0 0.6 pad.4
  135.7 8.2 %all-to-all-done.6 = f32[32,1,2048]{2,1,0:T(1,128)S(1)} async-done(((f32[32,1,2048]{2,1,0:T(1,128)}), f32[32,1,2048]{2,1,0:T(1,128)S(1)}, u32[]{:S(2)}, u32[]{:S(2)}) %all-to-all-start.6) | async-done | bytes 262176 | tf_op jit(solution)/shard_map/all_to_all | solution.py:166
  143.9 7.0 %all-to-all-start.5 = ((bf16[32,8,128]{2,1,0:T(8,128)(2,1)}), bf16[32,8,128]{2,1,0:T(8,128)(2,1)S(1)}, u32[]{:S(2)}, u32[]{:S(2)}) async-start(bf16[32,8,128]{2,1,0:T(8,128)(2,1)} %pad.4), calls=%async_computation.5 | async-start | bytes 131072 | tf_op jit(solution)/shard_map/all_to_all | solution.py:191
  150.9 1.2 pad_maximum_fusion
  152.2 0.7 reshape.112
  152.9 13.9 %all-to-all-done.5.ret = bf16[32,8,128]{2,1,0:T(8,128)(2,1)S(1)} async-done(((bf16[32,8,128]{2,1,0:T(8,128)(2,1)}), bf16[32,8,128]{2,1,0:T(8,128)(2,1)S(1)}, u32[]{:S(2)}, u32[]{:S(2)}) %all-to-all-start.5) | async-done | bytes 65568 | tf_op jit(solution)/shard_map/all_to_all | solution.py:191
  166.8 0.6 copy-done.10
  167.4 1.9 %combine.1 = bf16[64,256]{1,0:T(8,128)(2,1)} custom-call(bf16[32,8,128]{2,1,0:T(8,128)(2,1)} %copy-done.10, s32[1,256]{1,0:T(1,128)} %bitcast.102, bf16[32,256]{1,0:T(8,128)(2,1)} %copy-done.11, bf16[32,64]{1,0:T(8,128)(2,1)} %bitcast.106), custom_call_target="tpu_custom_call" | custom-call | tf_op jit(solution)/shard_map/combine/pallas_call | solution.py:199
  (70 shorter events, 7.5 us)
Async XLA Ops:
  0.6 91.1 %copy-start = (bf16[1,160,2048]{2,1,0:T(8,128)(2,1)S(1)}, bf16[1,160,2048]{2,1,0:T(8,128)(2,1)}, u32[]{:S(2)}) copy-start(bf16[1,160,2048]{2,1,0:T(8,128)(2,1)} %param.14) | copy-start | bytes 1966084
  75.9 1.5 copy-start.1
  77.3 11.3 %collective-permute-start = (bf16[16,41,8,128]{3,2,1,0:T(8,128)(2,1)S(1)}, bf16[16,41,8,128]{3,2,1,0:T(8,128)(2,1)}, u32[]{:S(2)}, u32[]{:S(2)}) collective-permute-start(bf16[16,41,8,128]{3,2,1,0:T(8,128)(2,1)S(1)} %bitcast.87), channel_id=1, source_target_pairs={{0,32},{32,0},{1,33},{33,1},{2,34},{34,2},{3,35},{35,3},{4,36},{36... | collective-permute-start | bytes 4030472 | tf_op jit(solution)/shard_map/ppermute | solution.py:156
  85.8 1.7 %copy-start.6 = (bf16[32,4096]{1,0:T(8,128)(2,1)S(1)}, bf16[32,4096]{1,0:T(8,128)(2,1)}, u32[]{:S(2)}) copy-start(bf16[32,4096]{1,0:T(8,128)(2,1)} %reshape.102) | copy-start | bytes 786436
  85.8 1.8 %copy-start.2 = (bf16[1,2,160,2048]{3,2,1,0:T(8,128)(2,1)S(1)}, bf16[1,2,160,2048]{3,2,1,0:T(8,128)(2,1)}, u32[]{:S(2)}) copy-start(bf16[1,2,160,2048]{3,2,1,0:T(8,128)(2,1)} %param.13) | copy-start | bytes 3932164
  87.6 2.1 %copy-start.3 = (bf16[160,4096]{1,0:T(8,128)(2,1)}, bf16[160,4096]{1,0:T(8,128)(2,1)S(1)}, u32[]{:S(2)}) copy-start(bf16[160,4096]{1,0:T(8,128)(2,1)S(1)} %constant_dynamic-update-slice_fusion) | copy-start | bytes 3932164
  92.1 0.7 copy-start.7
  92.9 2.4 %copy-start.4 = (bf16[160,4096]{1,0:T(8,128)(2,1)S(1)}, bf16[160,4096]{1,0:T(8,128)(2,1)}, u32[]{:S(2)}) copy-start(bf16[160,4096]{1,0:T(8,128)(2,1)} %copy-done.3) | copy-start | bytes 3932164
  92.9 2.4 %copy-start.15 = (f32[160,160]{1,0:T(8,128)S(1)}, f32[160,160]{1,0:T(8,128)}, u32[]{:S(2)}) copy-start(f32[160,160]{1,0:T(8,128)} %fusion.16) | copy-start | bytes 307204
  93.2 4.1 %collective-permute-start.1 = (bf16[160,2048]{1,0:T(8,128)(2,1)S(1)}, bf16[160,2048]{1,0:T(8,128)(2,1)S(1)}, u32[]{:S(2)}, u32[]{:S(2)}) collective-permute-start(bf16[160,2048]{1,0:T(8,128)(2,1)S(1)} %fusion), channel_id=1, source_target_pairs={{0,32},{32,0},{1,33},{33,1},{2,34},{34,2},{3,35},{35,3},{4,36},{36... | collective-permute-start | bytes 1966088 | tf_op jit(solution)/shard_map/ppermute | solution.py:177
  98.6 14.3 %all-to-all-start.3 = ((bf16[4,40,2048]{2,1,0:T(8,128)(2,1)}), bf16[4,40,2048]{2,1,0:T(8,128)(2,1)S(1)}, u32[]{:S(2)}, u32[]{:S(2)}) async-start(bf16[4,40,2048]{2,1,0:T(8,128)(2,1)} %pad_maximum_fusion.2), calls=%async_computation.3 | async-start | bytes 1310720 | tf_op jit(solution)/shard_map/all_to_all | solution.py:184
  102.1 16.4 %copy-start.9 = (f32[256,32]{0,1:T(8,128)S(1)}, f32[256,32]{0,1:T(8,128)}, u32[]{:S(2)}) copy-start(f32[256,32]{0,1:T(8,128)} %param.11) | copy-start | bytes 98308
  102.1 16.4 %copy-start.13 = (s32[256,1]{0,1:T(1,128)S(1)}, s32[256,1]{0,1:T(1,128)}, u32[]{:S(2)}) copy-start(s32[256,1]{0,1:T(1,128)} %param.12) | copy-start | bytes 3076
  102.1 16.3 %copy-start.14 = (f32[1,256]{1,0:T(1,128)S(1)}, f32[1,256]{1,0:T(1,128)}, u32[]{:S(2)}) copy-start(f32[1,256]{1,0:T(1,128)} %get-tuple-element.6) | copy-start | bytes 3076
  102.2 16.5 %copy-start.12 = (bf16[256,64]{0,1:T(8,128)(2,1)S(1)}, bf16[256,64]{0,1:T(8,128)(2,1)}, u32[]{:S(2)}) copy-start(bf16[256,64]{0,1:T(8,128)(2,1)} %param.8) | copy-start | bytes 98308
  113.0 19.6 %copy-start.5 = (bf16[160,4096]{1,0:T(8,128)(2,1)S(1)}, bf16[160,4096]{1,0:T(8,128)(2,1)}, u32[]{:S(2)}) copy-start(bf16[160,4096]{1,0:T(8,128)(2,1)} %copy-done.3) | copy-start | bytes 3932164
  113.9 12.2 %all-to-all-start.4 = ((bf16[4,10,2048]{2,1,0:T(8,128)(2,1)}), bf16[4,10,2048]{2,1,0:T(8,128)(2,1)S(1)}, u32[]{:S(2)}, u32[]{:S(2)}) async-start(bf16[4,10,2048]{2,1,0:T(8,128)(2,1)} %pad_maximum_fusion.3), calls=%async_computation.4 | async-start | bytes 524288 | tf_op jit(solution)/shard_map/all_to_all | solution.py:188
  118.7 14.4 %copy-start.11 = (bf16[32,256]{1,0:T(8,128)(2,1)}, bf16[32,256]{1,0:T(8,128)(2,1)S(1)}, u32[]{:S(2)}) copy-start(bf16[32,256]{1,0:T(8,128)(2,1)S(1)} %multiply_convert_fusion.2.lg) | copy-start | bytes 49156
  126.9 17.0 %all-to-all-start.6 = ((f32[32,1,2048]{2,1,0:T(1,128)}), f32[32,1,2048]{2,1,0:T(1,128)S(1)}, u32[]{:S(2)}, u32[]{:S(2)}) async-start(f32[32,1,2048]{2,1,0:T(1,128)} %broadcast_in_dim.16), calls=%async_computation.6 | async-start | bytes 524288 | tf_op jit(solution)/shard_map/all_to_all | solution.py:166
  133.4 0.9 copy-start.8
  143.9 22.9 %all-to-all-start.5 = ((bf16[32,8,128]{2,1,0:T(8,128)(2,1)}), bf16[32,8,128]{2,1,0:T(8,128)(2,1)S(1)}, u32[]{:S(2)}, u32[]{:S(2)}) async-start(bf16[32,8,128]{2,1,0:T(8,128)(2,1)} %pad.4), calls=%async_computation.5 | async-start | bytes 131072 | tf_op jit(solution)/shard_map/all_to_all | solution.py:191
  166.8 0.6 copy-start.10

commit v2 on v1

v2 whole, which is shorter than its diff:
```python
import jax
import jax.numpy as jnp
from jax import lax
from jax.experimental import pallas as pl
from jax.experimental.pallas import tpu as pltpu
from jax.sharding import Mesh, PartitionSpec as P


ZL, X, CORE, Y, ZH = 4, 4, 2, 8, 4
EX = ("y", "zh")
DP = ("zl", "x", "core")
E = 32
CAP = 10
T = 256
F = 64
D = 2048
KT = 2 * D // 128
AUX = 0.2
ROOT = 0.7978845608028654
CUBE = 0.044715
GROUPS = ZL * X
SENT = KT + KT // 4 + 1
BACK = KT // 2 + KT // 8
TILES = ZL * BACK + 4
HID = 160
BUNDLE = 3 * HID + 16
WIDE = D + 512
DISPATCH_KIB = 60000
CROSS = GROUPS * CAP + E
F32, BF16 = jnp.float32, jnp.bfloat16
CONTRACT_LAST = (((1,), (1,)), ((), ()))
CONTRACT_FIRST = (((0,), (0,)), ((), ()))


def vmem(n):
    return [pl.BlockSpec(memory_space=pltpu.VMEM)] * n


def iota(shape, dim):
    return lax.broadcasted_iota(jnp.int32, shape, dim)


def slots(idx):
    hit = iota((E, T), 0) == idx
    hot = jnp.where(hit, 1.0, 0.0).astype(F32)
    earlier = jnp.where(iota((T, T), 0) < iota((T, T), 1), 1.0, 0.0).astype(BF16)
    before = jnp.dot(hot.astype(BF16), earlier, preferred_element_type=F32)
    return hot, jnp.sum(hot * before, axis=0, keepdims=True)


def dispatch_kernel(tok_h, og_h, eo_h, pt_h, idx_h, out, tile, tok, og, eo, pt, ix, sems):
    copies = [
        pltpu.make_async_copy(a, b, sems.at[i])
        for i, (a, b) in enumerate(
            (
                (idx_h, ix),
                (tok_h, tok),
                (og_h, og),
                (pt_h, pt),
                (eo_h, eo),
            )
        )
    ]
    for c in copies:
        c.start()
    copies[0].wait()
    idx = ix[...]
    hot, slot = slots(idx)
    row = iota((E * 16, T), 0)
    sel = jnp.where(
        (lax.shift_right_logical(row, 4) == idx) & (lax.bitwise_and(row, 15) == slot.astype(jnp.int32)),
        1.0,
        0.0,
    ).astype(BF16)
    wide = jnp.where(iota((128, T), 0) == idx, 1.0, 0.0).astype(BF16)
    counts = lax.dot_general(jnp.ones((8, T), BF16), wide, CONTRACT_LAST, preferred_element_type=F32)
    tile[...] = counts.astype(BF16)
    for c in copies[1:]:
        c.wait()
    gate = jnp.sum(pt[...] * hot, axis=0, keepdims=True)
    grad = og[...].astype(F32)
    gated = (gate * grad).astype(BF16)
    dot = jnp.sum(grad * eo[...].astype(F32), axis=0, keepdims=True)
    both = jnp.concatenate([tok[...], gated], axis=0)
    sent = lax.dot_general(sel, both, CONTRACT_LAST, preferred_element_type=F32)
    h0 = dot.astype(BF16).astype(F32)
    h1 = (dot - h0).astype(BF16).astype(F32)
    h2 = dot - h0 - h1
    line = iota((16, 128), 0)
    extra = jnp.zeros((16, 128), F32)
    for i, h in enumerate((h0, h1, h2)):
        for j in range(2):
            extra = extra + jnp.where(line == CAP + 2 * i + j, h[:, 128 * j : 128 * (j + 1)], 0.0)
    out[...] = (sent.reshape(E, 16, 128) + extra[None]).astype(BF16)


def bundle_kernel(in_h, down_h, tile_h, out, tile, sems):
    copies = [
        pltpu.make_async_copy(a, b, sems.at[i])
        for i, (a, b) in enumerate(
            (
                (tile_h, tile),
                (in_h.at[0], out.at[pl.ds(0, HID)]),
                (in_h.at[1], out.at[pl.ds(HID, HID)]),
                (down_h, out.at[pl.ds(2 * HID, HID)]),
            )
        )
    ]
    for c in copies:
        c.start()
    out[3 * HID :, :] = jnp.zeros((BUNDLE - 3 * HID, D), BF16)
    copies[0].wait()
    out[3 * HID :, :128] = jnp.concatenate([tile[...], tile[...]], axis=0)
    for c in copies[1:]:
        c.wait()


def pack_kernel(got, tile, partner, out, dot_ref):
    low = iota((16, 128), 1) < F
    line = iota((8, 128), 0)
    tail = [jnp.zeros((8, 128), F32) for _ in range(KT // 4)]
    total = jnp.zeros((16, 128), F32)
    for j in range(E // 2):
        a = got[2 * j].astype(F32)
        b = got[2 * j + 1].astype(F32)
        total = total + a + b
        t = jnp.where(low, a, pltpu.roll(b, F, 1))
        g = jnp.where(low, pltpu.roll(a, F, 1), b)
        for k, v in ((j, t), (j + E // 2, g)):
            out[k] = v[:8].astype(BF16)
            i = k % 4
            rest = v[8:] if i == 0 else pltpu.roll(v[8:], 2 * i, 0)
            tail[k // 4] = jnp.where((line >= 2 * i) & (line < 2 * i + 2), rest, tail[k // 4])
    for m in range(KT // 4):
        out[KT + m] = tail[m].astype(BF16)
    pair = tile[...].astype(F32) + partner[3 * HID : 3 * HID + 8, :128].astype(F32)
    out[KT + KT // 4] = pair.astype(BF16)
    odd = lax.bitwise_and(line, 1)
    for h in range(2):
        pick = jnp.where((line >= 2) & (odd == h), total[8:], 0.0)
        dot_ref[:, 128 * h : 128 * (h + 1)] = jnp.sum(pick, axis=0, keepdims=True)


def spread():
    a, b = iota((128, 128), 0), iota((128, 128), 1)
    group = lax.bitwise_and(lax.shift_right_logical(a, 1), 15)
    want = 8 * group + 2 * lax.shift_right_logical(a, 5) + lax.bitwise_and(a, 1)
    return jnp.where(b == want, 1.0, 0.0)


def unpack(src, tok, dy):
    perm = spread().astype(BF16)
    for k in range(KT):
        dst, at = (tok, k) if k < KT // 2 else (dy, k - KT // 2)
        block = src[:, k].astype(F32).reshape(GROUPS * 8, 128).astype(BF16)
        dst[: GROUPS * 8, 128 * at : 128 * (at + 1)] = block
    for m in range(KT // 4):
        block = src[:, KT + m].astype(F32).reshape(GROUPS * 8, 128).astype(BF16)
        lines = jnp.dot(perm, block, preferred_element_type=F32).astype(BF16)
        for i in range(4):
            k = 4 * m + i
            dst, at = (tok, k) if k < KT // 2 else (dy, k - KT // 2)
            dst[GROUPS * 8 : GROUPS * CAP, 128 * at : 128 * (at + 1)] = lines[32 * i : 32 * (i + 1)]


def hidden_grads(tok, dy, w):
    rows = tok[:, :D]
    gate_pre = lax.dot_general(rows, w[:HID], CONTRACT_LAST, preferred_element_type=F32)
    up_pre = lax.dot_general(rows, w[HID : 2 * HID], CONTRACT_LAST, preferred_element_type=F32)
    hidden = lax.dot_general(dy[...], w[2 * HID : 3 * HID], CONTRACT_LAST, preferred_element_type=F32)
    square = gate_pre * gate_pre
    th = jnp.tanh(ROOT * (gate_pre + CUBE * square * gate_pre))
    half = 0.5 * (1.0 + th)
    slope = half + 0.5 * gate_pre * (1.0 - th * th) * (ROOT * (1.0 + 3.0 * CUBE * square))
    return (hidden * up_pre * slope).astype(BF16), (hidden * (gate_pre * half)).astype(BF16)


def split_lanes(v):
    high = v.astype(BF16).astype(F32)
    return jnp.where(iota(v.shape, 1) < F, high, v - high).astype(BF16)


def main_kernel(src, mine, other, dot_ref, pt_ref, idx_ref, tok_in, out, cross, gg_ref, ug_ref, lg_ref, dy):
    unpack(src, cross, dy)
    gg, ug = hidden_grads(cross, dy, mine)
    gg_o, ug_o = hidden_grads(cross, dy, other)
    gg_ref[...] = gg
    ug_ref[...] = ug
    cross[:, D : D + HID] = gg_o
    cross[:, D + 256 : D + 256 + HID] = ug_o
    perm = spread().astype(BF16)
    for m in range(KT // 8):
        cols = pl.ds(512 * m, 512)
        part = jnp.dot(gg, mine[:HID, cols], preferred_element_type=F32)
        part = part + jnp.dot(ug, mine[HID : 2 * HID, cols], preferred_element_type=F32)
        part = part + jnp.dot(gg_o, other[:HID, cols], preferred_element_type=F32)
        part = part + jnp.dot(ug_o, other[HID : 2 * HID, cols], preferred_element_type=F32)
        lines = []
        for i in range(4):
            block = part[:, 128 * i : 128 * (i + 1)]
            head = block[: GROUPS * 8].reshape(X, ZL, 8, 128).astype(BF16)
            for z in range(ZL):
                out[:, z * BACK + 4 * m + i] = head[:, z]
            lines.append(block[GROUPS * 8 :])
        tails = jnp.concatenate(lines, axis=0).astype(BF16)
        tails = lax.dot_general(perm, tails, CONTRACT_FIRST, preferred_element_type=F32)
        tails = tails.reshape(X, ZL, 8, 128).astype(BF16)
        for z in range(ZL):
            out[:, z * BACK + KT // 2 + m] = tails[:, z]
    count = jnp.sum(src[:, SENT - 1].astype(F32), axis=0)
    diagonal = iota((E, 128), 0) == iota((E, 128), 1)
    counts = jnp.sum(jnp.where(diagonal, count[:1], 0.0), axis=1, keepdims=True)
    pt = pt_ref[...]
    hot = jnp.where(iota((E, T), 0) == idx_ref[...], 1.0, 0.0)
    grad = hot * dot_ref[...] + AUX * E * counts / (T * E)
    lg = (pt * (grad - jnp.sum(pt * grad, axis=0, keepdims=True))).astype(BF16)
    lg_ref[...] = lg
    twice = jnp.concatenate([tok_in[...], tok_in[...]], axis=0)
    pair = split_lanes(lax.dot_general(lg, twice, CONTRACT_LAST, preferred_element_type=F32))
    for i in range(4):
        for x in range(X):
            out[x, ZL * BACK + i] = pair[8 * i : 8 * (i + 1)]


def merged(got, i):
    pair = jnp.sum(got[:, pl.ds(i, 4)].astype(F32), axis=0).reshape(E, 128)
    return pair + pltpu.roll(pair, F, 1)


def middle_kernel(got, out):
    for z in range(ZL):
        for k in range(BACK):
            out[z, k] = jnp.sum(got[:, z * BACK + k].astype(F32), axis=0).astype(BF16)
    pair = split_lanes(merged(got, ZL * BACK))
    for z in range(ZL):
        for i in range(4):
            out[z, BACK + i] = pair[8 * i : 8 * (i + 1)]


def sum_kernel(got, cross, out, bundle, router):
    low = iota((8, 128), 1) < F
    line = iota((8, 128), 0)

    def total(k):
        return jnp.sum(got[:, k].astype(F32), axis=0)

    for m in range(KT // 8):
        tail = total(KT // 2 + m)
        for i in range(4):
            k = 4 * m + i
            head = total(k)
            rest = tail if i == 0 else pltpu.roll(tail, 8 - 2 * i, 0)
            rest = jnp.where(line < 2, rest, 0.0)
            out[2 * k] = jnp.where(low, head, pltpu.roll(rest, F, 1)).astype(BF16)
            out[2 * k + 1] = jnp.where(low, pltpu.roll(head, F, 1), rest).astype(BF16)
    share = merged(got, BACK)
    router[...] = share
    bundle[: GROUPS * CAP, :] = cross[...]
    bundle[GROUPS * CAP :, :] = jnp.zeros((E, WIDE), BF16)
    bundle[GROUPS * CAP :, :128] = split_lanes(share)


def weight_kernel(mine, came, gg, ug, share, out, router):
    n = GROUPS * CAP
    for i, m in enumerate((gg, ug)):
        o = came[:n, D + 256 * i : D + 256 * i + HID]
        for c in range(D // 512):
            cols = pl.ds(512 * c, 512)
            grad = lax.dot_general(m[...], mine[:n, cols], CONTRACT_FIRST, preferred_element_type=F32)
            grad = grad + lax.dot_general(o, came[:n, cols], CONTRACT_FIRST, preferred_element_type=F32)
            out[i, :, cols] = grad.astype(BF16)
    pair = came[n:, :128].astype(F32)
    router[...] = (share[...] + pair + pltpu.roll(pair, F, 1))[:, :F]


def combine_kernel(ret, idx_ref, lg, rw, out):
    idx = idx_ref[...]
    _, slot = slots(idx)
    slot = slot.astype(jnp.int32)
    row = iota((E * 8, T), 0)
    mine = lax.shift_right_logical(row, 3) == idx
    c = lax.bitwise_and(row, 7)
    r = ret[...].reshape(E * 8, 128)
    acc = lax.dot_general(rw[...], lg[...], CONTRACT_FIRST, preferred_element_type=F32)
    for h in range(2):
        sel = jnp.where(mine & (c + 8 * h == slot), 1.0, 0.0).astype(BF16)
        p = lax.dot_general(r, sel, CONTRACT_FIRST, preferred_element_type=F32)
        acc = acc + p[F * h : F * (h + 1)]
    out[...] = acc.astype(BF16)


def local(kernel, outs, ins, flops, scratch=(), hbm=False, kib=8192):
    one = not isinstance(outs, tuple)
    return pl.pallas_call(
        kernel,
        out_shape=outs,
        in_specs=[pl.BlockSpec(memory_space=pltpu.HBM)] * len(ins) if hbm else vmem(len(ins)),
        out_specs=vmem(1)[0] if one else tuple(vmem(len(outs))),
        scratch_shapes=list(scratch),
        cost_estimate=pl.CostEstimate(flops=flops, bytes_accessed=0, transcendentals=0),
        compiler_params=pltpu.CompilerParams(vmem_limit_bytes=kib * 1024),
    )(*ins)


def shape(*dims, dtype=BF16):
    return jax.ShapeDtypeStruct(dims, dtype)


def per_device(tokens, out_grad, expert_out, probs, idx, in_weight, down_weight, router_weight):
    return layer(
        tokens.T,
        out_grad.T,
        expert_out.T,
        probs.T,
        idx.T,
        in_weight,
        down_weight,
        router_weight,
    )


def layer(tok, og, eo, pt, ix, in_weight, down_weight, router_weight):
    swap = [(0, 1), (1, 0)]
    send, tile = local(
        dispatch_kernel,
        (shape(E, 16, 128), shape(8, 128)),
        (tok, og, eo, pt, ix),
        10**7,
        (
            pltpu.VMEM((F, T), BF16),
            pltpu.VMEM((F, T), BF16),
            pltpu.VMEM((F, T), BF16),
            pltpu.VMEM((E, T), F32),
            pltpu.VMEM((1, T), jnp.int32),
            pltpu.SemaphoreType.DMA((5,)),
        ),
        hbm=True,
        kib=DISPATCH_KIB,
    )
    got = lax.all_to_all(send, EX, 0, 0, tiled=True)
    mine = local(
        bundle_kernel,
        shape(BUNDLE, D),
        (in_weight[0], down_weight[0], tile),
        10**6,
        (pltpu.VMEM((8, 128), BF16), pltpu.SemaphoreType.DMA((4,))),
        hbm=True,
        kib=60000,
    )
    other = lax.ppermute(mine, "core", swap)
    packed, gate_dot = local(pack_kernel, (shape(SENT, 8, 128), shape(1, T, dtype=F32)), (got, tile, other), 10**7)
    line = lax.all_to_all(jnp.broadcast_to(packed, (ZL, *packed.shape)), "zl", 0, 0, tiled=True)
    plane = lax.all_to_all(jnp.broadcast_to(line, (X, *line.shape)), "x", 0, 0, tiled=True)
    own = plane.reshape(GROUPS, SENT, 8, 128)
    rows = GROUPS * CAP
    work = 10 * rows * HID * D
    back, cross, gg, ug, lg = local(
        main_kernel,
        (shape(X, TILES, 8, 128), shape(rows, WIDE), shape(rows, HID), shape(rows, HID), shape(E, T)),
        (own, mine, other, gate_dot, pt, ix, tok),
        2 * work,
        (pltpu.VMEM((rows, D), BF16),),
        kib=20000,
    )
    landed = lax.all_to_all(back, "x", 0, 0, tiled=True)
    onward = local(middle_kernel, shape(ZL, BACK + 4, 8, 128), (landed,), 10**6)
    landed = lax.all_to_all(onward, "zl", 0, 0, tiled=True)
    rows_back, bundle, share = local(
        sum_kernel, (shape(E, 8, 128), shape(CROSS, WIDE), shape(E, 128, dtype=F32)), (landed, cross), 10**6
    )
    ret = lax.all_to_all(rows_back, EX, 0, 0, tiled=True)
    came = lax.ppermute(bundle, "core", swap)
    weights, router_sum = local(
        weight_kernel, (shape(2, HID, D), shape(E, F, dtype=F32)), (bundle, came, gg, ug, share), work, kib=12000
    )
    token_grad = local(combine_kernel, shape(F, T), (ret, ix, lg, router_weight.T), 10**7)
    return token_grad.T, weights[None], router_sum.T


def solution(mesh):
    fine = Mesh(mesh.devices.reshape(ZL, X, CORE, Y, ZH), DP + EX)
    in_specs = (
        P(DP, EX),
        P(DP, EX),
        P(DP, EX),
        P(DP, None),
        P(DP, None),
        P(EX, None, DP, None),
        P(EX, DP, None),
        P(EX, None),
    )
    out_specs = (P(DP, EX), P(EX, None, DP, None), P(EX, None))
    return jax.shard_map(
        per_device, mesh=fine, in_specs=in_specs, out_specs=out_specs, check_vma=False
    )
```

time: 170 us -> 139 us (0.82)
  waiting for transfers between devices: 39.4 us -> 0.01 us
  blocking collectives: 71 us -> 104 us
  local copies, waits for them, and re-layouts: 11.2 us -> 0.26 us
  starting transfers between devices: 30.3 us -> 22.7 us
  matrix products: 5.7 us -> 0 us
  Pallas kernels: 5.59 us -> 10.6 us
  other arithmetic: 4.97 us -> 0 us
    all_to_all x4 -> x0, waiting for transfers between devices: 38.4 us -> none  [the longest x1 13.9 us: per_device(): ret = lax.all_to_all(back, EX, 0, 0, tiled=True)]
    all_to_all x3 -> x6, blocking collectives: 71 us -> 104 us  [the longest x1 27.4 us: layer(): got = lax.all_to_all(send, EX, 0, 0, tiled=True)]
    all_to_all x4 -> x0, starting transfers between devices: 20.9 us -> none  [the longest x1 7 us: per_device(): ret = lax.all_to_all(back, EX, 0, 0, tiled=True)]
    ppermute x2, starting transfers between devices: 9.47 us -> 22.7 us  [the longest x1 16 us: layer(): other = lax.ppermute(mine, 'core', swap)]
    dot_general x15 -> x0, matrix products: 5.7 us -> none  [the longest x2 1.43 us: backward(): lax.dot_general(tok, in_w[0], CONTRACT_LAST, preferred_element_type=F32)]
    pallas_call x3 -> x8, Pallas kernels: 5.59 us -> 10.6 us  [local(): pl.pallas_call(kernel, out_shape=outs, in_specs=[pl.BlockSpec(memory_spac...]
    unnamed x35 -> x14, local copies, waits for them, and re-layouts: 4.41 us -> 0.04 us
    reshape x10 -> x0, local copies, waits for them, and re-layouts: 3.44 us -> none  [the longest x1 1.3 us: rows_of(): head = got[:, :KT].transpose(0, 2, 1, 3).reshape(n * 8, 2 * D)]
  transfers between devices with their start and end apart: 6 -> 2, of which waited for: 5 -> 0; matrix products, arithmetic and copies ran while one was open for 7% -> 0% of each run, Pallas kernels for 0% -> 1%
where the time goes in v2:
time: 139 us; the launch traced here: 138 us
  blocking collectives  104 us (75%)
  starting transfers between devices  22.7 us (16%)
  Pallas kernels  10.6 us (8%)
    all_to_all x1, blocking collectives, layer(): got = lax.all_to_all(send, EX, 0, 0, tiled=True)  27.4 us
    all_to_all x1, blocking collectives, layer(): ret = lax.all_to_all(rows_back, EX, 0, 0, tiled=True)  20.8 us
    all_to_all x1, blocking collectives, layer(): lax.all_to_all(jnp.broadcast_to(line, (X, *line.shape)), 'x', 0, 0, tiled...  19.6 us
    ppermute x1, starting transfers between devices, layer(): other = lax.ppermute(mine, 'core', swap)  16 us
    all_to_all x1, blocking collectives, layer(): lax.all_to_all(jnp.broadcast_to(packed, (ZL, *packed.shape)), 'zl', 0, 0,...  14.6 us
    all_to_all x1, blocking collectives, layer(): landed = lax.all_to_all(onward, 'zl', 0, 0, tiled=True)  11.5 us
    pallas_call x8, Pallas kernels, local(): pl.pallas_call(kernel, out_shape=outs, in_specs=[pl.BlockSpec(memory_spac...  10.6 us
    all_to_all x1, blocking collectives, layer(): landed = lax.all_to_all(back, 'x', 0, 0, tiled=True)  10.2 us
  transfers between devices with their start and end apart: 2, of which 0 were waited for; matrix products, arithmetic and copies ran while one was open for 0% of the time, Pallas kernels for 1%

profile of v2, /device:TPU:1, one launch (start us, length us, event | category | flops | bytes accessed | tf_op | source)
XLA Modules:
  0.0 138.4 jit_solution(11368403146292757009)
XLA Ops:
  0.6 1.9 %shard_map.103 = (bf16[32,16,128]{2,1,0:T(8,128)(2,1)}, bf16[8,128]{1,0:T(8,128)(2,1)}) custom-call(bf16[64,256]{1,0:T(8,128)(2,1)} %bitcast.13, bf16[64,256]{1,0:T(8,128)(2,1)} %bitcast.23, bf16[64,256]{1,0:T(8,128)(2,1)} %bitcast.24, f32[32,256]{1,0:T(8,128)} %bitcast.15, s32[1,256]{1,0:T(1,128)} %bitcast.17), custom_call_target="tpu_custom_call" | custom-call | flops 10000000 | tf_op jit(solution)/shard_map/pallas_call | solution.py:294
  2.5 0.0 copy-start.6
  2.5 0.0 copy-start.4
  2.5 2.9 %shard_map.104.mine = bf16[496,2048]{1,0:T(8,128)(2,1)} custom-call(bf16[2,160,2048]{2,1,0:T(8,128)(2,1)} %bitcast.21, bf16[160,2048]{1,0:T(8,128)(2,1)} %bitcast.22, bf16[8,128]{1,0:T(8,128)(2,1)} %get-tuple-element.18.tile_h.tile), custom_call_target="tpu_custom_call" | custom-call | flops 1000000 | tf_op jit(solution)/shard_map/pallas_call | solution.py:294
  5.4 16.0 %collective-permute-start = (bf16[496,2048]{1,0:T(8,128)(2,1)}, bf16[496,2048]{1,0:T(8,128)(2,1)S(1)}, u32[]{:S(2)}, u32[]{:S(2)}) collective-permute-start(bf16[496,2048]{1,0:T(8,128)(2,1)} %shard_map.104.mine), channel_id=1, source_target_pairs={{0,32},{32,0},{1,33},{33,1},{2,34},{34,2},{3,35},{35,3},{4,36},{36... | collective-permute-start | bytes 6094856 | tf_op jit(solution)/shard_map/ppermute | solution.py:350
  21.4 0.0 copy-done.6
  21.4 27.4 %all_to_all.30.got = bf16[32,16,128]{2,1,0:T(8,128)(2,1)S(1)} all-to-all(bf16[32,16,128]{2,1,0:T(8,128)(2,1)S(1)} %copy-done.6), channel_id=1, replica_groups=mesh['zl'=4,'x'=4,'core'=2,'y'=8,'zh'=4] {'y','zh'}, dimensions={0} | all-to-all | bytes 262144 | tf_op jit(solution)/shard_map/all_to_all | solution.py:340
  48.8 0.0 collective-permute-done.partner.other
  48.8 0.0 copy-done.4
  48.9 0.1 shard_map.105
  49.0 14.6 %all_to_all.31 = bf16[4,41,8,128]{3,2,1,0:T(8,128)(2,1)S(1)} all-to-all(bf16[4,41,8,128]{3,2,1,0:T(8,128)(2,1)S(1)} %broadcast_in_dim.9), channel_id=1, replica_groups=mesh['zl'=4,'x'=4,'core'=2,'y'=8,'zh'=4] {'zl'}, dimensions={0} | all-to-all | bytes 671744 | tf_op jit(solution)/shard_map/all_to_all | solution.py:352
  63.6 0.2 broadcast_in_dim.10
  63.8 0.0 copy-start
  63.8 0.0 copy-start.1
  63.8 0.0 copy-start.2
  63.8 0.0 copy-start.3
  63.9 19.6 %all_to_all.32 = bf16[4,4,41,8,128]{4,3,2,1,0:T(8,128)(2,1)S(1)} all-to-all(bf16[4,4,41,8,128]{4,3,2,1,0:T(8,128)(2,1)S(1)} %broadcast_in_dim.10), channel_id=1, replica_groups=mesh['zl'=4,'x'=4,'core'=2,'y'=8,'zh'=4] {'x'}, dimensions={0} | all-to-all | bytes 2686976 | tf_op jit(solution)/shard_map/all_to_all | solution.py:353
  83.5 0.0 copy-done
  83.5 0.0 copy-done.1
  83.5 0.0 copy-done.2
  83.5 0.0 copy-done.3
  83.5 2.6 %shard_map.106 = (bf16[4,84,8,128]{3,2,1,0:T(8,128)(2,1)S(1)}, bf16[160,2560]{1,0:T(8,128)(2,1)S(1)}, bf16[160,160]{1,0:T(8,128)(2,1)S(1)}, bf16[160,160]{1,0:T(8,128)(2,1)S(1)}, bf16[32,256]{1,0:T(8,128)(2,1)S(1)}) custom-call(bf16[16,41,8,128]{3,2,1,0:T(8,128)(2,1)S(1)} %bitcast.12, bf16[496,2048]{1,0:T(8,128)(2,1)S(1)} %copy-done, ...), custom_call_target="tpu_custom_call" | custom-call | flops 1048576000 | tf_op jit(solution)/shard_map/pallas_call | solution.py:294
  86.1 10.2 %all_to_all.33.got = bf16[4,84,8,128]{3,2,1,0:T(8,128)(2,1)S(1)} all-to-all(bf16[4,84,8,128]{3,2,1,0:T(8,128)(2,1)S(1)} %get-tuple-element.21), channel_id=1, replica_groups=mesh['zl'=4,'x'=4,'core'=2,'y'=8,'zh'=4] {'x'}, dimensions={0} | all-to-all | bytes 1376256 | tf_op jit(solution)/shard_map/all_to_all | solution.py:365
  96.3 0.1 shard_map.107
  96.4 11.5 %all_to_all.34.got = bf16[4,24,8,128]{3,2,1,0:T(8,128)(2,1)S(1)} all-to-all(bf16[4,24,8,128]{3,2,1,0:T(8,128)(2,1)S(1)} %shard_map.107), channel_id=1, replica_groups=mesh['zl'=4,'x'=4,'core'=2,'y'=8,'zh'=4] {'zl'}, dimensions={0} | all-to-all | bytes 393216 | tf_op jit(solution)/shard_map/all_to_all | solution.py:367
  107.9 0.1 shard_map.108
  108.0 6.7 %collective-permute-start.1 = (bf16[192,2560]{1,0:T(8,128)(2,1)S(1)}, bf16[192,2560]{1,0:T(8,128)(2,1)S(1)}, u32[]{:S(2)}, u32[]{:S(2)}) collective-permute-start(bf16[192,2560]{1,0:T(8,128)(2,1)S(1)} %get-tuple-element.25.mine), channel_id=1, source_target_pairs={{0,32},{32,0},{1,33},{33,1},{2,34},{34,2},{3,35},{35,3},{4,36},{36... | collective-permute-start | bytes 2949128 | tf_op jit(solution)/shard_map/ppermute | solution.py:372
  114.7 20.8 %all_to_all.35.ret = bf16[32,8,128]{2,1,0:T(8,128)(2,1)S(1)} all-to-all(bf16[32,8,128]{2,1,0:T(8,128)(2,1)S(1)} %get-tuple-element.23), channel_id=1, replica_groups=mesh['zl'=4,'x'=4,'core'=2,'y'=8,'zh'=4] {'y','zh'}, dimensions={0} | all-to-all | bytes 131072 | tf_op jit(solution)/shard_map/all_to_all | solution.py:371
  135.5 0.0 copy-done.5
  135.5 1.0 shard_map.109
  136.5 0.0 collective-permute-done.1.came
  136.5 1.9 %shard_map.110 = (bf16[2,160,2048]{2,1,0:T(8,128)(2,1)}, f32[32,64]{1,0:T(8,128)}) custom-call(bf16[192,2560]{1,0:T(8,128)(2,1)S(1)} %get-tuple-element.25.mine, bf16[192,2560]{1,0:T(8,128)(2,1)S(1)} %collective-permute-done.1.came, bf16[160,160]{1,0:T(8,128)(2,1)S(1)} %get-tuple-element.26.gg, bf16[160,160]{1,0:T(8,128)(2,1)S(1)} %get-tuple-element.27.ug, ...), custom_call_target="tpu_custom_call" | custom-call | flops 524288000 | tf_op jit(solution)/shard_map/pallas_call | solution.py:294
  (2 shorter events, 0.0 us)
Async XLA Ops:
  2.5 19.0 %copy-start.6 = (bf16[32,16,128]{2,1,0:T(8,128)(2,1)S(1)}, bf16[32,16,128]{2,1,0:T(8,128)(2,1)}, u32[]{:S(2)}) copy-start(bf16[32,16,128]{2,1,0:T(8,128)(2,1)} %get-tuple-element.17) | copy-start | bytes 393220
  2.5 46.3 %copy-start.4 = (bf16[8,128]{1,0:T(8,128)(2,1)S(1)}, bf16[8,128]{1,0:T(8,128)(2,1)}, u32[]{:S(2)}) copy-start(bf16[8,128]{1,0:T(8,128)(2,1)} %get-tuple-element.18.tile_h.tile) | copy-start | bytes 6148
  5.4 43.4 %collective-permute-start = (bf16[496,2048]{1,0:T(8,128)(2,1)}, bf16[496,2048]{1,0:T(8,128)(2,1)S(1)}, u32[]{:S(2)}, u32[]{:S(2)}) collective-permute-start(bf16[496,2048]{1,0:T(8,128)(2,1)} %shard_map.104.mine), channel_id=1, source_target_pairs={{0,32},{32,0},{1,33},{33,1},{2,34},{34,2},{3,35},{35,3},{4,36},{36... | collective-permute-start | bytes 6094856 | tf_op jit(solution)/shard_map/ppermute | solution.py:350
  63.8 19.7 %copy-start = (bf16[496,2048]{1,0:T(8,128)(2,1)S(1)}, bf16[496,2048]{1,0:T(8,128)(2,1)}, u32[]{:S(2)}) copy-start(bf16[496,2048]{1,0:T(8,128)(2,1)} %shard_map.104.mine) | copy-start | bytes 6094852
  63.8 19.7 %copy-start.1 = (bf16[256,64]{0,1:T(8,128)(2,1)S(1)}, bf16[256,64]{0,1:T(8,128)(2,1)}, u32[]{:S(2)}) copy-start(bf16[256,64]{0,1:T(8,128)(2,1)} %param.8) | copy-start | bytes 98308
  63.8 19.7 %copy-start.2 = (f32[256,32]{0,1:T(8,128)S(1)}, f32[256,32]{0,1:T(8,128)}, u32[]{:S(2)}) copy-start(f32[256,32]{0,1:T(8,128)} %param.11) | copy-start | bytes 98308
  63.8 19.7 %copy-start.3 = (s32[256,1]{0,1:T(1,128)S(1)}, s32[256,1]{0,1:T(1,128)}, u32[]{:S(2)}) copy-start(s32[256,1]{0,1:T(1,128)} %param.12) | copy-start | bytes 3076
  96.3 39.2 %copy-start.5 = (bf16[64,32]{0,1:T(8,128)(2,1)S(1)}, bf16[64,32]{0,1:T(8,128)(2,1)}, u32[]{:S(2)}) copy-start(bf16[64,32]{0,1:T(8,128)(2,1)} %param.15) | copy-start | bytes 12292
  108.0 28.5 %collective-permute-start.1 = (bf16[192,2560]{1,0:T(8,128)(2,1)S(1)}, bf16[192,2560]{1,0:T(8,128)(2,1)S(1)}, u32[]{:S(2)}, u32[]{:S(2)}) collective-permute-start(bf16[192,2560]{1,0:T(8,128)(2,1)S(1)} %get-tuple-element.25.mine), channel_id=1, source_target_pairs={{0,32},{32,0},{1,33},{33,1},{2,34},{34,2},{3,35},{35,3},{4,36},{36... | collective-permute-start | bytes 2949128 | tf_op jit(solution)/shard_map/ppermute | solution.py:372

commit v3 on v2

--- a/solution.py
+++ b/solution.py
@@ -227,40 +227,31 @@
     return pair + pltpu.roll(pair, F, 1)
 
 
-def middle_kernel(got, out):
-    for z in range(ZL):
-        for k in range(BACK):
-            out[z, k] = jnp.sum(got[:, z * BACK + k].astype(F32), axis=0).astype(BF16)
-    pair = split_lanes(merged(got, ZL * BACK))
-    for z in range(ZL):
-        for i in range(4):
-            out[z, BACK + i] = pair[8 * i : 8 * (i + 1)]
-
-
-def sum_kernel(got, cross, out, bundle, router):
+def middle_kernel(got, cross, out, bundle, share_ref):
     low = iota((8, 128), 1) < F
     line = iota((8, 128), 0)
-
-    def total(k):
-        return jnp.sum(got[:, k].astype(F32), axis=0)
-
-    for m in range(KT // 8):
-        tail = total(KT // 2 + m)
-        for i in range(4):
-            k = 4 * m + i
-            head = total(k)
-            rest = tail if i == 0 else pltpu.roll(tail, 8 - 2 * i, 0)
-            rest = jnp.where(line < 2, rest, 0.0)
-            out[2 * k] = jnp.where(low, head, pltpu.roll(rest, F, 1)).astype(BF16)
-            out[2 * k + 1] = jnp.where(low, pltpu.roll(head, F, 1), rest).astype(BF16)
-    share = merged(got, BACK)
-    router[...] = share
+    for z in range(ZL):
+
+        def total(k):
+            return jnp.sum(got[:, z * BACK + k].astype(F32), axis=0)
+
+        for m in range(KT // 8):
+            tail = total(KT // 2 + m)
+            for i in range(4):
+                k = 4 * m + i
+                head = total(k)
+                rest = tail if i == 0 else pltpu.roll(tail, 8 - 2 * i, 0)
+                rest = jnp.where(line < 2, rest, 0.0)
+                out[E * z + 2 * k] = jnp.where(low, head, pltpu.roll(rest, F, 1)).astype(BF16)
+                out[E * z + 2 * k + 1] = jnp.where(low, pltpu.roll(head, F, 1), rest).astype(BF16)
+    share = merged(got, ZL * BACK)
+    share_ref[...] = share
     bundle[: GROUPS * CAP, :] = cross[...]
     bundle[GROUPS * CAP :, :] = jnp.zeros((E, WIDE), BF16)
     bundle[GROUPS * CAP :, :128] = split_lanes(share)
 
 
-def weight_kernel(mine, came, gg, ug, share, out, router):
+def weight_kernel(mine, came, gg, ug, out):
     n = GROUPS * CAP
     for i, m in enumerate((gg, ug)):
         o = came[:n, D + 256 * i : D + 256 * i + HID]
@@ -269,8 +260,23 @@
             grad = lax.dot_general(m[...], mine[:n, cols], CONTRACT_FIRST, preferred_element_type=F32)
             grad = grad + lax.dot_general(o, came[:n, cols], CONTRACT_FIRST, preferred_element_type=F32)
             out[i, :, cols] = grad.astype(BF16)
-    pair = came[n:, :128].astype(F32)
-    router[...] = (share[...] + pair + pltpu.roll(pair, F, 1))[:, :F]
+
+
+def folded(a, b):
+    pair = a.astype(F32) + b.astype(F32)
+    return pair + pltpu.roll(pair, F, 1)
+
+
+def cores_kernel(share, came, out):
+    out[...] = split_lanes(share[...] + folded(came[GROUPS * CAP :, :128], jnp.zeros((E, 128), F32)))
+
+
+def pairs_kernel(a, b, out):
+    out[...] = split_lanes(folded(a[...], b[...]))
+
+
+def router_kernel(a, b, out):
+    out[...] = folded(a[...], b[...])[:, :F]
 
 
 def combine_kernel(ret, idx_ref, lg, rw, out):
@@ -280,12 +286,18 @@
     row = iota((E * 8, T), 0)
     mine = lax.shift_right_logical(row, 3) == idx
     c = lax.bitwise_and(row, 7)
-    r = ret[...].reshape(E * 8, 128)
+    r = ret[pl.ds(0, E)].astype(F32)
+    for z in range(1, ZL):
+        r = r + ret[pl.ds(E * z, E)].astype(F32)
+    high = r.astype(BF16)
+    low = (r - high.astype(F32)).astype(BF16)
     acc = lax.dot_general(rw[...], lg[...], CONTRACT_FIRST, preferred_element_type=F32)
     for h in range(2):
         sel = jnp.where(mine & (c + 8 * h == slot), 1.0, 0.0).astype(BF16)
-        p = lax.dot_general(r, sel, CONTRACT_FIRST, preferred_element_type=F32)
-        acc = acc + p[F * h : F * (h + 1)]
+        for part in (high, low):
+            lanes = part.reshape(E * 8, 128)
+            p = lax.dot_general(lanes, sel, CONTRACT_FIRST, preferred_element_type=F32)
+            acc = acc + p[F * h : F * (h + 1)]
     out[...] = acc.astype(BF16)
 
 
@@ -363,17 +375,18 @@
         kib=20000,
     )
     landed = lax.all_to_all(back, "x", 0, 0, tiled=True)
-    onward = local(middle_kernel, shape(ZL, BACK + 4, 8, 128), (landed,), 10**6)
-    landed = lax.all_to_all(onward, "zl", 0, 0, tiled=True)
     rows_back, bundle, share = local(
-        sum_kernel, (shape(E, 8, 128), shape(CROSS, WIDE), shape(E, 128, dtype=F32)), (landed, cross), 10**6
-    )
-    ret = lax.all_to_all(rows_back, EX, 0, 0, tiled=True)
+        middle_kernel, (shape(ZL * E, 8, 128), shape(CROSS, WIDE), shape(E, 128, dtype=F32)), (landed, cross), 10**6
+    )
+    ret = lax.all_to_all(rows_back, ("zl", *EX), 0, 0, tiled=True)
     came = lax.ppermute(bundle, "core", swap)
-    weights, router_sum = local(
-        weight_kernel, (shape(2, HID, D), shape(E, F, dtype=F32)), (bundle, came, gg, ug, share), work, kib=12000
-    )
+    pair = local(cores_kernel, shape(E, 128), (share, came), 10**5)
+    got = lax.ppermute(pair, "zl", [(0, 1), (1, 0), (2, 3), (3, 2)])
+    weights = local(weight_kernel, shape(2, HID, D), (bundle, came, gg, ug), work, kib=12000)
+    pair = local(pairs_kernel, shape(E, 128), (pair, got), 10**5)
+    got = lax.ppermute(pair, "zl", [(0, 2), (2, 0), (1, 3), (3, 1)])
     token_grad = local(combine_kernel, shape(F, T), (ret, ix, lg, router_weight.T), 10**7)
+    router_sum = local(router_kernel, shape(E, F, dtype=F32), (pair, got), 10**5)
     return token_grad.T, weights[None], router_sum.T
 
 

time: 139 us -> 137 us (0.986); the launches traced: 138 us -> 135 us
  blocking collectives: 104 us -> 71.8 us
  starting transfers between devices: 22.7 us -> 40.4 us
  waiting for transfers between devices: 0.01 us -> 9.32 us
  Pallas kernels: 10.6 us -> 12.2 us
    all_to_all x2 -> x0, blocking collectives: 32.2 us -> none  [the longest x1 20.8 us: layer(): ret = lax.all_to_all(rows_back, EX, 0, 0, tiled=True)]
    all_to_all x0 -> x1, starting transfers between devices: none -> 9.97 us  [layer(): ret = lax.all_to_all(rows_back, ('zl', *EX), 0, 0, tiled=True)]
    ppermute x0 -> x2, starting transfers between devices: none -> 7.81 us  [the longest x1 5.24 us: layer(): got = lax.ppermute(pair, 'zl', [(0, 2), (2, 0), (1, 3), (3, 1)])]
    ppermute x0 -> x2, waiting for transfers between devices: none -> 5.63 us  [the longest x1 5.63 us: layer(): got = lax.ppermute(pair, 'zl', [(0, 1), (1, 0), (2, 3), (3, 2)])]
    all_to_all x0 -> x1, waiting for transfers between devices: none -> 3.68 us  [layer(): ret = lax.all_to_all(rows_back, ('zl', *EX), 0, 0, tiled=True)]
    pallas_call x8 -> x10, Pallas kernels: 10.6 us -> 12.2 us  [local(): pl.pallas_call(kernel, out_shape=outs, in_specs=[pl.BlockSpec(memory_spac...]
  transfers between devices with their start and end apart: 2 -> 5, of which waited for: 0 -> 2; matrix products, arithmetic and copies ran while one was open for 0% -> 0% of each run, Pallas kernels for 1% -> 2%
where the time goes in v3:
time: 137 us; the launch traced here: 135 us
  blocking collectives  71.8 us (52%)
  starting transfers between devices  40.4 us (29%)
  Pallas kernels  12.2 us (9%)
  waiting for transfers between devices  9.32 us (7%)
    all_to_all x1, blocking collectives, layer(): got = lax.all_to_all(send, EX, 0, 0, tiled=True)  27.4 us
    all_to_all x1, blocking collectives, layer(): lax.all_to_all(jnp.broadcast_to(line, (X, *line.shape)), 'x', 0, 0, tiled...  19.6 us
    ppermute x1, starting transfers between devices, layer(): other = lax.ppermute(mine, 'core', swap)  16 us
    all_to_all x1, blocking collectives, layer(): lax.all_to_all(jnp.broadcast_to(packed, (ZL, *packed.shape)), 'zl', 0, 0,...  14.6 us
    pallas_call x10, Pallas kernels, local(): pl.pallas_call(kernel, out_shape=outs, in_specs=[pl.BlockSpec(memory_spac...  12.2 us
    all_to_all x1, blocking collectives, layer(): landed = lax.all_to_all(back, 'x', 0, 0, tiled=True)  10.2 us
    all_to_all x1, starting transfers between devices, layer(): ret = lax.all_to_all(rows_back, ('zl', *EX), 0, 0, tiled=True)  9.97 us
    ppermute x1, starting transfers between devices, layer(): came = lax.ppermute(bundle, 'core', swap)  6.57 us
  transfers between devices with their start and end apart: 5, of which 2 were waited for; matrix products, arithmetic and copies ran while one was open for 0% of the time, Pallas kernels for 2%

profile of v3, /device:TPU:1, one launch (start us, length us, event | category | flops | bytes accessed | tf_op | source)
XLA Modules:
  0.0 134.8 jit_solution(9916871285498991558)
XLA Ops:
  0.6 1.9 %shard_map.103 = (bf16[32,16,128]{2,1,0:T(8,128)(2,1)}, bf16[8,128]{1,0:T(8,128)(2,1)}) custom-call(bf16[64,256]{1,0:T(8,128)(2,1)} %bitcast.13, bf16[64,256]{1,0:T(8,128)(2,1)} %bitcast.25, bf16[64,256]{1,0:T(8,128)(2,1)} %bitcast.26, f32[32,256]{1,0:T(8,128)} %bitcast.15, s32[1,256]{1,0:T(1,128)} %bitcast.17), custom_call_target="tpu_custom_call" | custom-call | flops 10000000 | tf_op jit(solution)/shard_map/pallas_call | solution.py:306
  2.5 0.0 copy-start.6
  2.5 0.0 copy-start.4
  2.5 2.9 %shard_map.104.mine = bf16[496,2048]{1,0:T(8,128)(2,1)} custom-call(bf16[2,160,2048]{2,1,0:T(8,128)(2,1)} %bitcast.21, bf16[160,2048]{1,0:T(8,128)(2,1)} %bitcast.23, bf16[8,128]{1,0:T(8,128)(2,1)} %get-tuple-element.16.tile_h.tile), custom_call_target="tpu_custom_call" | custom-call | flops 1000000 | tf_op jit(solution)/shard_map/pallas_call | solution.py:306
  5.4 16.0 %collective-permute-start = (bf16[496,2048]{1,0:T(8,128)(2,1)}, bf16[496,2048]{1,0:T(8,128)(2,1)S(1)}, u32[]{:S(2)}, u32[]{:S(2)}) collective-permute-start(bf16[496,2048]{1,0:T(8,128)(2,1)} %shard_map.104.mine), channel_id=1, source_target_pairs={{0,32},{32,0},{1,33},{33,1},{2,34},{34,2},{3,35},{35,3},{4,36},{36... | collective-permute-start | bytes 6094856 | tf_op jit(solution)/shard_map/ppermute | solution.py:362
  21.4 27.4 %all_to_all.25.got = bf16[32,16,128]{2,1,0:T(8,128)(2,1)S(1)} all-to-all(bf16[32,16,128]{2,1,0:T(8,128)(2,1)S(1)} %copy-done.6), channel_id=1, replica_groups=mesh['zl'=4,'x'=4,'core'=2,'y'=8,'zh'=4] {'y','zh'}, dimensions={0} | all-to-all | bytes 262144 | tf_op jit(solution)/shard_map/all_to_all | solution.py:352
  48.8 0.0 collective-permute-done.partner.other
  48.8 0.1 shard_map.105
  49.0 14.6 %all_to_all.26 = bf16[4,41,8,128]{3,2,1,0:T(8,128)(2,1)S(1)} all-to-all(bf16[4,41,8,128]{3,2,1,0:T(8,128)(2,1)S(1)} %broadcast_in_dim.9), channel_id=1, replica_groups=mesh['zl'=4,'x'=4,'core'=2,'y'=8,'zh'=4] {'zl'}, dimensions={0} | all-to-all | bytes 671744 | tf_op jit(solution)/shard_map/all_to_all | solution.py:364
  63.6 0.2 broadcast_in_dim.10
  63.8 0.0 copy-start.1
  63.8 0.0 copy-start.2
  63.8 0.0 copy-start.3
  63.9 19.6 %all_to_all.27 = bf16[4,4,41,8,128]{4,3,2,1,0:T(8,128)(2,1)S(1)} all-to-all(bf16[4,4,41,8,128]{4,3,2,1,0:T(8,128)(2,1)S(1)} %broadcast_in_dim.10), channel_id=1, replica_groups=mesh['zl'=4,'x'=4,'core'=2,'y'=8,'zh'=4] {'x'}, dimensions={0} | all-to-all | bytes 2686976 | tf_op jit(solution)/shard_map/all_to_all | solution.py:365
  83.5 0.0 copy-done
  83.5 2.6 %shard_map.106 = (bf16[4,84,8,128]{3,2,1,0:T(8,128)(2,1)S(1)}, bf16[160,2560]{1,0:T(8,128)(2,1)S(1)}, bf16[160,160]{1,0:T(8,128)(2,1)S(1)}, bf16[160,160]{1,0:T(8,128)(2,1)S(1)}, bf16[32,256]{1,0:T(8,128)(2,1)S(1)}) custom-call(bf16[16,41,8,128]{3,2,1,0:T(8,128)(2,1)S(1)} %bitcast.12, bf16[496,2048]{1,0:T(8,128)(2,1)S(1)} %copy-done, ...), custom_call_target="tpu_custom_call" | custom-call | flops 1048576000 | tf_op jit(solution)/shard_map/pallas_call | solution.py:306
  86.1 10.2 %all_to_all.28.got = bf16[4,84,8,128]{3,2,1,0:T(8,128)(2,1)S(1)} all-to-all(bf16[4,84,8,128]{3,2,1,0:T(8,128)(2,1)S(1)} %get-tuple-element.19), channel_id=1, replica_groups=mesh['zl'=4,'x'=4,'core'=2,'y'=8,'zh'=4] {'x'}, dimensions={0} | all-to-all | bytes 1376256 | tf_op jit(solution)/shard_map/all_to_all | solution.py:377
  96.3 0.9 shard_map.107
  97.2 6.6 %collective-permute-start.1 = (bf16[192,2560]{1,0:T(8,128)(2,1)S(1)}, bf16[192,2560]{1,0:T(8,128)(2,1)S(1)}, u32[]{:S(2)}, u32[]{:S(2)}) collective-permute-start(bf16[192,2560]{1,0:T(8,128)(2,1)S(1)} %get-tuple-element.23.mine), channel_id=1, source_target_pairs={{0,32},{32,0},{1,33},{33,1},{2,34},{34,2},{3,35},{35,3},{4,36},{36... | collective-permute-start | bytes 2949128 | tf_op jit(solution)/shard_map/ppermute | solution.py:382
  103.8 10.0 %all-to-all-start.4 = ((bf16[128,8,128]{2,1,0:T(8,128)(2,1)}), bf16[128,8,128]{2,1,0:T(8,128)(2,1)S(1)}, u32[]{:S(2)}, u32[]{:S(2)}) async-start(bf16[128,8,128]{2,1,0:T(8,128)(2,1)} %get-tuple-element.21), calls=%async_computation.4 | async-start | bytes 524288 | tf_op jit(solution)/shard_map/all_to_all | solution.py:381
  113.8 0.0 collective-permute-done.1.came
  113.8 0.1 shard_map.110.a
  113.9 2.6 %collective-permute-start.2 = (bf16[32,128]{1,0:T(8,128)(2,1)S(1)}, bf16[32,128]{1,0:T(8,128)(2,1)S(1)}, u32[]{:S(2)}, u32[]{:S(2)}) collective-permute-start(bf16[32,128]{1,0:T(8,128)(2,1)S(1)} %shard_map.110.a), channel_id=1, source_target_pairs={{0,256},{256,0},{512,768},{768,512},{1,257},{257,1},{513,769},{769... | collective-permute-start | bytes 24584 | tf_op jit(solution)/shard_map/ppermute | solution.py:384
  116.4 5.6 %collective-permute-done.2.b = bf16[32,128]{1,0:T(8,128)(2,1)S(1)} collective-permute-done((bf16[32,128]{1,0:T(8,128)(2,1)S(1)}, bf16[32,128]{1,0:T(8,128)(2,1)S(1)}, u32[]{:S(2)}, u32[]{:S(2)}) %collective-permute-start.2) | collective-permute-done | bytes 8224 | tf_op jit(solution)/shard_map/ppermute | solution.py:384
  122.1 0.1 shard_map.111.a
  122.1 5.2 %collective-permute-start.3 = (bf16[32,128]{1,0:T(8,128)(2,1)S(1)}, bf16[32,128]{1,0:T(8,128)(2,1)S(1)}, u32[]{:S(2)}, u32[]{:S(2)}) collective-permute-start(bf16[32,128]{1,0:T(8,128)(2,1)S(1)} %shard_map.111.a), channel_id=1, source_target_pairs={{0,512},{512,0},{256,768},{768,256},{1,513},{513,1},{257,769},{769... | collective-permute-start | bytes 24584 | tf_op jit(solution)/shard_map/ppermute | solution.py:387
  127.4 0.0 copy-start.5
  127.4 1.9 %shard_map.109 = bf16[2,160,2048]{2,1,0:T(8,128)(2,1)} custom-call(bf16[192,2560]{1,0:T(8,128)(2,1)S(1)} %get-tuple-element.23.mine, bf16[192,2560]{1,0:T(8,128)(2,1)S(1)} %collective-permute-done.1.came, bf16[160,160]{1,0:T(8,128)(2,1)S(1)} %get-tuple-element.24.gg, bf16[160,160]{1,0:T(8,128)(2,1)S(1)} %get-tuple-element.25.ug), custom_call_target="tpu_custom_call" | custom-call | flops 524288000 | tf_op jit(solution)/shard_map/pallas_call | solution.py:306
  129.3 0.0 collective-permute-done.3.b
  129.3 0.7 shard_map.112
  130.0 3.7 %all-to-all-done.4.ret = bf16[128,8,128]{2,1,0:T(8,128)(2,1)S(1)} async-done(((bf16[128,8,128]{2,1,0:T(8,128)(2,1)}), bf16[128,8,128]{2,1,0:T(8,128)(2,1)S(1)}, u32[]{:S(2)}, u32[]{:S(2)}) %all-to-all-start.4) | async-done | bytes 262176 | tf_op jit(solution)/shard_map/all_to_all | solution.py:381
  133.7 1.1 shard_map.108
  (8 shorter events, 0.1 us)
Async XLA Ops:
  2.5 18.9 %copy-start.6 = (bf16[32,16,128]{2,1,0:T(8,128)(2,1)S(1)}, bf16[32,16,128]{2,1,0:T(8,128)(2,1)}, u32[]{:S(2)}) copy-start(bf16[32,16,128]{2,1,0:T(8,128)(2,1)} %get-tuple-element.15) | copy-start | bytes 393220
  2.5 46.3 %copy-start.4 = (bf16[8,128]{1,0:T(8,128)(2,1)S(1)}, bf16[8,128]{1,0:T(8,128)(2,1)}, u32[]{:S(2)}) copy-start(bf16[8,128]{1,0:T(8,128)(2,1)} %get-tuple-element.16.tile_h.tile) | copy-start | bytes 6148
  5.4 43.4 %collective-permute-start = (bf16[496,2048]{1,0:T(8,128)(2,1)}, bf16[496,2048]{1,0:T(8,128)(2,1)S(1)}, u32[]{:S(2)}, u32[]{:S(2)}) collective-permute-start(bf16[496,2048]{1,0:T(8,128)(2,1)} %shard_map.104.mine), channel_id=1, source_target_pairs={{0,32},{32,0},{1,33},{33,1},{2,34},{34,2},{3,35},{35,3},{4,36},{36... | collective-permute-start | bytes 6094856 | tf_op jit(solution)/shard_map/ppermute | solution.py:362
  63.8 19.7 %copy-start = (bf16[496,2048]{1,0:T(8,128)(2,1)S(1)}, bf16[496,2048]{1,0:T(8,128)(2,1)}, u32[]{:S(2)}) copy-start(bf16[496,2048]{1,0:T(8,128)(2,1)} %shard_map.104.mine) | copy-start | bytes 6094852
  63.8 19.7 %copy-start.1 = (bf16[256,64]{0,1:T(8,128)(2,1)S(1)}, bf16[256,64]{0,1:T(8,128)(2,1)}, u32[]{:S(2)}) copy-start(bf16[256,64]{0,1:T(8,128)(2,1)} %param.8) | copy-start | bytes 98308
  63.8 19.7 %copy-start.2 = (f32[256,32]{0,1:T(8,128)S(1)}, f32[256,32]{0,1:T(8,128)}, u32[]{:S(2)}) copy-start(f32[256,32]{0,1:T(8,128)} %param.11) | copy-start | bytes 98308
  63.8 19.7 %copy-start.3 = (s32[256,1]{0,1:T(1,128)S(1)}, s32[256,1]{0,1:T(1,128)}, u32[]{:S(2)}) copy-start(s32[256,1]{0,1:T(1,128)} %param.12) | copy-start | bytes 3076
  97.2 16.6 %collective-permute-start.1 = (bf16[192,2560]{1,0:T(8,128)(2,1)S(1)}, bf16[192,2560]{1,0:T(8,128)(2,1)S(1)}, u32[]{:S(2)}, u32[]{:S(2)}) collective-permute-start(bf16[192,2560]{1,0:T(8,128)(2,1)S(1)} %get-tuple-element.23.mine), channel_id=1, source_target_pairs={{0,32},{32,0},{1,33},{33,1},{2,34},{34,2},{3,35},{35,3},{4,36},{36... | collective-permute-start | bytes 2949128 | tf_op jit(solution)/shard_map/ppermute | solution.py:382
  103.8 29.9 %all-to-all-start.4 = ((bf16[128,8,128]{2,1,0:T(8,128)(2,1)}), bf16[128,8,128]{2,1,0:T(8,128)(2,1)S(1)}, u32[]{:S(2)}, u32[]{:S(2)}) async-start(bf16[128,8,128]{2,1,0:T(8,128)(2,1)} %get-tuple-element.21), calls=%async_computation.4 | async-start | bytes 524288 | tf_op jit(solution)/shard_map/all_to_all | solution.py:381
  113.9 8.2 %collective-permute-start.2 = (bf16[32,128]{1,0:T(8,128)(2,1)S(1)}, bf16[32,128]{1,0:T(8,128)(2,1)S(1)}, u32[]{:S(2)}, u32[]{:S(2)}) collective-permute-start(bf16[32,128]{1,0:T(8,128)(2,1)S(1)} %shard_map.110.a), channel_id=1, source_target_pairs={{0,256},{256,0},{512,768},{768,512},{1,257},{257,1},{513,769},{769... | collective-permute-start | bytes 24584 | tf_op jit(solution)/shard_map/ppermute | solution.py:384
  122.1 7.2 %collective-permute-start.3 = (bf16[32,128]{1,0:T(8,128)(2,1)S(1)}, bf16[32,128]{1,0:T(8,128)(2,1)S(1)}, u32[]{:S(2)}, u32[]{:S(2)}) collective-permute-start(bf16[32,128]{1,0:T(8,128)(2,1)S(1)} %shard_map.111.a), channel_id=1, source_target_pairs={{0,512},{512,0},{256,768},{768,256},{1,513},{513,1},{257,769},{769... | collective-permute-start | bytes 24584 | tf_op jit(solution)/shard_map/ppermute | solution.py:387
  127.4 6.3 %copy-start.5 = (bf16[64,32]{0,1:T(8,128)(2,1)S(1)}, bf16[64,32]{0,1:T(8,128)(2,1)}, u32[]{:S(2)}) copy-start(bf16[64,32]{0,1:T(8,128)(2,1)} %param.15) | copy-start | bytes 12292

commit v4 on v3

--- a/solution.py
+++ b/solution.py
@@ -6,8 +6,8 @@
 from jax.sharding import Mesh, PartitionSpec as P
 
 
-ZL, X, CORE, Y, ZH = 4, 4, 2, 8, 4
-EX = ("y", "zh")
+ZL, X, CORE = 4, 4, 2
+EX = "expert"
 DP = ("zl", "x", "core")
 E = 32
 CAP = 10
@@ -25,6 +25,7 @@
 HID = 160
 BUNDLE = 3 * HID + 16
 WIDE = D + 512
+FROM_LAST = list(range(E))[::-1]
 DISPATCH_KIB = 60000
 CROSS = GROUPS * CAP + E
 F32, BF16 = jnp.float32, jnp.bfloat16
@@ -68,7 +69,8 @@
     hot, slot = slots(idx)
     row = iota((E * 16, T), 0)
     sel = jnp.where(
-        (lax.shift_right_logical(row, 4) == idx) & (lax.bitwise_and(row, 15) == slot.astype(jnp.int32)),
+        (E - 1 - lax.shift_right_logical(row, 4) == idx)
+        & (lax.bitwise_and(row, 15) == slot.astype(jnp.int32)),
         1.0,
         0.0,
     ).astype(BF16)
@@ -121,8 +123,8 @@
     tail = [jnp.zeros((8, 128), F32) for _ in range(KT // 4)]
     total = jnp.zeros((16, 128), F32)
     for j in range(E // 2):
-        a = got[2 * j].astype(F32)
-        b = got[2 * j + 1].astype(F32)
+        a = got[E - 1 - 2 * j].astype(F32)
+        b = got[E - 2 - 2 * j].astype(F32)
         total = total + a + b
         t = jnp.where(low, a, pltpu.roll(b, F, 1))
         g = jnp.where(low, pltpu.roll(a, F, 1), b)
@@ -275,11 +277,8 @@
     out[...] = split_lanes(folded(a[...], b[...]))
 
 
-def router_kernel(a, b, out):
-    out[...] = folded(a[...], b[...])[:, :F]
-
-
-def combine_kernel(ret, idx_ref, lg, rw, out):
+def combine_kernel(ret, idx_ref, lg, rw, pair, far, out, router):
+    router[...] = folded(pair[...], far[...])[:, :F]
     idx = idx_ref[...]
     _, slot = slots(idx)
     slot = slot.astype(jnp.int32)
@@ -349,7 +348,7 @@
         hbm=True,
         kib=DISPATCH_KIB,
     )
-    got = lax.all_to_all(send, EX, 0, 0, tiled=True)
+    got = lax.all_to_all(send, EX, 0, 0, tiled=True, axis_index_groups=[FROM_LAST])
     mine = local(
         bundle_kernel,
         shape(BUNDLE, D),
@@ -378,20 +377,21 @@
     rows_back, bundle, share = local(
         middle_kernel, (shape(ZL * E, 8, 128), shape(CROSS, WIDE), shape(E, 128, dtype=F32)), (landed, cross), 10**6
     )
-    ret = lax.all_to_all(rows_back, ("zl", *EX), 0, 0, tiled=True)
+    ret = lax.all_to_all(rows_back, ("zl", EX), 0, 0, tiled=True)
     came = lax.ppermute(bundle, "core", swap)
     pair = local(cores_kernel, shape(E, 128), (share, came), 10**5)
     got = lax.ppermute(pair, "zl", [(0, 1), (1, 0), (2, 3), (3, 2)])
     weights = local(weight_kernel, shape(2, HID, D), (bundle, came, gg, ug), work, kib=12000)
     pair = local(pairs_kernel, shape(E, 128), (pair, got), 10**5)
     got = lax.ppermute(pair, "zl", [(0, 2), (2, 0), (1, 3), (3, 1)])
-    token_grad = local(combine_kernel, shape(F, T), (ret, ix, lg, router_weight.T), 10**7)
-    router_sum = local(router_kernel, shape(E, F, dtype=F32), (pair, got), 10**5)
+    token_grad, router_sum = local(
+        combine_kernel, (shape(F, T), shape(E, F, dtype=F32)), (ret, ix, lg, router_weight.T, pair, got), 10**7
+    )
     return token_grad.T, weights[None], router_sum.T
 
 
 def solution(mesh):
-    fine = Mesh(mesh.devices.reshape(ZL, X, CORE, Y, ZH), DP + EX)
+    fine = Mesh(mesh.devices.reshape(ZL, X, CORE, E), (*DP, EX))
     in_specs = (
         P(DP, EX),
         P(DP, EX),

time: 137 us -> 135 us (0.985)
  blocking collectives: 71.8 us -> 65.8 us
  starting transfers between devices: 40.4 us -> 44.3 us
    all_to_all x1, blocking collectives: 27.4 us -> 21 us  [layer(): lax.all_to_all(send, EX, 0, 0, tiled=True, axis_index_groups=[FROM_LAST])]
    all_to_all x1, starting transfers between devices: 9.97 us -> 13.9 us  [layer(): ret = lax.all_to_all(rows_back, ('zl', EX), 0, 0, tiled=True)]
    pallas_call x10 -> x9, Pallas kernels: 12.2 us -> 11.5 us  [local(): pl.pallas_call(kernel, out_shape=outs, in_specs=[pl.BlockSpec(memory_spac...]
where the time goes in v4:
time: 135 us; the launch traced here: 133 us
  blocking collectives  65.8 us (49%)
  starting transfers between devices  44.3 us (33%)
  Pallas kernels  11.5 us (9%)
  waiting for transfers between devices  10 us (7%)
    all_to_all x1, blocking collectives, layer(): lax.all_to_all(send, EX, 0, 0, tiled=True, axis_index_groups=[FROM_LAST])  21 us
    all_to_all x1, blocking collectives, layer(): lax.all_to_all(jnp.broadcast_to(line, (X, *line.shape)), 'x', 0, 0, tiled...  19.6 us
    ppermute x1, starting transfers between devices, layer(): other = lax.ppermute(mine, 'core', swap)  16 us
    all_to_all x1, blocking collectives, layer(): lax.all_to_all(jnp.broadcast_to(packed, (ZL, *packed.shape)), 'zl', 0, 0,...  15 us
    all_to_all x1, starting transfers between devices, layer(): ret = lax.all_to_all(rows_back, ('zl', EX), 0, 0, tiled=True)  13.9 us
    pallas_call x9, Pallas kernels, local(): pl.pallas_call(kernel, out_shape=outs, in_specs=[pl.BlockSpec(memory_spac...  11.5 us
    all_to_all x1, blocking collectives, layer(): landed = lax.all_to_all(back, 'x', 0, 0, tiled=True)  10.2 us
    ppermute x1, starting transfers between devices, layer(): came = lax.ppermute(bundle, 'core', swap)  6.57 us
  transfers between devices with their start and end apart: 5, of which 2 were waited for; matrix products, arithmetic and copies ran while one was open for 0% of the time, Pallas kernels for 2%

profile of v4, /device:TPU:1, one launch (start us, length us, event | category | flops | bytes accessed | tf_op | source)
XLA Modules:
  0.0 132.7 jit_solution(5719686518518498604)
XLA Ops:
  0.6 1.9 %shard_map.103 = (bf16[32,16,128]{2,1,0:T(8,128)(2,1)}, bf16[8,128]{1,0:T(8,128)(2,1)}) custom-call(bf16[64,256]{1,0:T(8,128)(2,1)} %bitcast.13, bf16[64,256]{1,0:T(8,128)(2,1)} %bitcast.24, bf16[64,256]{1,0:T(8,128)(2,1)} %bitcast.25, f32[32,256]{1,0:T(8,128)} %bitcast.15, s32[1,256]{1,0:T(1,128)} %bitcast.17), custom_call_target="tpu_custom_call" | custom-call | flops 10000000 | tf_op jit(solution)/shard_map/pallas_call | solution.py:305
  2.5 0.0 copy-start.6
  2.5 0.0 copy-start.4
  2.5 2.9 %shard_map.104.mine = bf16[496,2048]{1,0:T(8,128)(2,1)} custom-call(bf16[2,160,2048]{2,1,0:T(8,128)(2,1)} %bitcast.21, bf16[160,2048]{1,0:T(8,128)(2,1)} %bitcast.23, bf16[8,128]{1,0:T(8,128)(2,1)} %get-tuple-element.18.tile_h.tile), custom_call_target="tpu_custom_call" | custom-call | flops 1000000 | tf_op jit(solution)/shard_map/pallas_call | solution.py:305
  5.4 16.0 %collective-permute-start = (bf16[496,2048]{1,0:T(8,128)(2,1)}, bf16[496,2048]{1,0:T(8,128)(2,1)S(1)}, u32[]{:S(2)}, u32[]{:S(2)}) collective-permute-start(bf16[496,2048]{1,0:T(8,128)(2,1)} %shard_map.104.mine), channel_id=1, source_target_pairs={{0,32},{32,0},{1,33},{33,1},{2,34},{34,2},{3,35},{35,3},{4,36},{36... | collective-permute-start | bytes 6094856 | tf_op jit(solution)/shard_map/ppermute | solution.py:361
  21.4 0.0 copy-done.6
  21.4 21.0 %all_to_all.25.got = bf16[32,16,128]{2,1,0:T(8,128)(2,1)S(1)} all-to-all(bf16[32,16,128]{2,1,0:T(8,128)(2,1)S(1)} %copy-done.6), channel_id=1, replica_groups={{31,30,29,28,27,26,25,24,23,22,21,20,19,18,17,16,15,14,13,12,11,10,9,8,..., dimensions={0} | all-to-all | bytes 262144 | tf_op jit(solution)/shard_map/all_to_all | solution.py:351
  42.4 0.0 collective-permute-done.partner.other
  42.4 0.0 copy-done.4
  42.4 0.1 shard_map.105
  42.6 15.0 %all_to_all.26 = bf16[4,41,8,128]{3,2,1,0:T(8,128)(2,1)S(1)} all-to-all(bf16[4,41,8,128]{3,2,1,0:T(8,128)(2,1)S(1)} %broadcast_in_dim.9), channel_id=1, replica_groups=mesh['zl'=4,'x'=4,'core'=2,'expert'=32] {'zl'}, dimensions={0} | all-to-all | bytes 671744 | tf_op jit(solution)/shard_map/all_to_all | solution.py:363
  57.6 0.2 broadcast_in_dim.10
  57.8 0.0 copy-start.1
  57.8 0.0 copy-start.2
  57.8 0.0 copy-start.3
  57.8 19.6 %all_to_all.27 = bf16[4,4,41,8,128]{4,3,2,1,0:T(8,128)(2,1)S(1)} all-to-all(bf16[4,4,41,8,128]{4,3,2,1,0:T(8,128)(2,1)S(1)} %broadcast_in_dim.10), channel_id=1, replica_groups=mesh['zl'=4,'x'=4,'core'=2,'expert'=32] {'x'}, dimensions={0} | all-to-all | bytes 2686976 | tf_op jit(solution)/shard_map/all_to_all | solution.py:364
  77.5 2.6 %shard_map.106 = (bf16[4,84,8,128]{3,2,1,0:T(8,128)(2,1)S(1)}, bf16[160,2560]{1,0:T(8,128)(2,1)S(1)}, bf16[160,160]{1,0:T(8,128)(2,1)S(1)}, bf16[160,160]{1,0:T(8,128)(2,1)S(1)}, bf16[32,256]{1,0:T(8,128)(2,1)S(1)}) custom-call(bf16[16,41,8,128]{3,2,1,0:T(8,128)(2,1)S(1)} %bitcast.12, bf16[496,2048]{1,0:T(8,128)(2,1)S(1)} %copy-done, ...), custom_call_target="tpu_custom_call" | custom-call | flops 1048576000 | tf_op jit(solution)/shard_map/pallas_call | solution.py:305
  80.1 10.2 %all_to_all.28.got = bf16[4,84,8,128]{3,2,1,0:T(8,128)(2,1)S(1)} all-to-all(bf16[4,84,8,128]{3,2,1,0:T(8,128)(2,1)S(1)} %get-tuple-element.21), channel_id=1, replica_groups=mesh['zl'=4,'x'=4,'core'=2,'expert'=32] {'x'}, dimensions={0} | all-to-all | bytes 1376256 | tf_op jit(solution)/shard_map/all_to_all | solution.py:376
  90.3 0.9 shard_map.107
  91.2 6.6 %collective-permute-start.1 = (bf16[192,2560]{1,0:T(8,128)(2,1)S(1)}, bf16[192,2560]{1,0:T(8,128)(2,1)S(1)}, u32[]{:S(2)}, u32[]{:S(2)}) collective-permute-start(bf16[192,2560]{1,0:T(8,128)(2,1)S(1)} %get-tuple-element.26.mine), channel_id=1, source_target_pairs={{0,32},{32,0},{1,33},{33,1},{2,34},{34,2},{3,35},{35,3},{4,36},{36... | collective-permute-start | bytes 2949128 | tf_op jit(solution)/shard_map/ppermute | solution.py:381
  97.8 13.9 %all-to-all-start.4 = ((bf16[128,8,128]{2,1,0:T(8,128)(2,1)}), bf16[128,8,128]{2,1,0:T(8,128)(2,1)S(1)}, u32[]{:S(2)}, u32[]{:S(2)}) async-start(bf16[128,8,128]{2,1,0:T(8,128)(2,1)} %get-tuple-element.23), calls=%async_computation.4 | async-start | bytes 524288 | tf_op jit(solution)/shard_map/all_to_all | solution.py:380
  111.7 0.0 collective-permute-done.1.came
  111.7 0.1 shard_map.108.a
  111.8 2.6 %collective-permute-start.2 = (bf16[32,128]{1,0:T(8,128)(2,1)S(1)}, bf16[32,128]{1,0:T(8,128)(2,1)S(1)}, u32[]{:S(2)}, u32[]{:S(2)}) collective-permute-start(bf16[32,128]{1,0:T(8,128)(2,1)S(1)} %shard_map.108.a), channel_id=1, source_target_pairs={{0,256},{256,0},{512,768},{768,512},{1,257},{257,1},{513,769},{769... | collective-permute-start | bytes 24584 | tf_op jit(solution)/shard_map/ppermute | solution.py:383
  114.4 5.6 %collective-permute-done.2.b = bf16[32,128]{1,0:T(8,128)(2,1)S(1)} collective-permute-done((bf16[32,128]{1,0:T(8,128)(2,1)S(1)}, bf16[32,128]{1,0:T(8,128)(2,1)S(1)}, u32[]{:S(2)}, u32[]{:S(2)}) %collective-permute-start.2) | collective-permute-done | bytes 8224 | tf_op jit(solution)/shard_map/ppermute | solution.py:383
  120.0 0.1 shard_map.109.pair
  120.1 5.2 %collective-permute-start.3 = (bf16[32,128]{1,0:T(8,128)(2,1)S(1)}, bf16[32,128]{1,0:T(8,128)(2,1)S(1)}, u32[]{:S(2)}, u32[]{:S(2)}) collective-permute-start(bf16[32,128]{1,0:T(8,128)(2,1)S(1)} %shard_map.109.pair), channel_id=1, source_target_pairs={{0,512},{512,0},{256,768},{768,256},{1,513},{513,1},{257,769},{769... | collective-permute-start | bytes 24584 | tf_op jit(solution)/shard_map/ppermute | solution.py:386
  125.3 0.0 copy-start.5
  125.3 1.9 %shard_map.111 = bf16[2,160,2048]{2,1,0:T(8,128)(2,1)} custom-call(bf16[192,2560]{1,0:T(8,128)(2,1)S(1)} %get-tuple-element.26.mine, bf16[192,2560]{1,0:T(8,128)(2,1)S(1)} %collective-permute-done.1.came, bf16[160,160]{1,0:T(8,128)(2,1)S(1)} %get-tuple-element.28.gg, bf16[160,160]{1,0:T(8,128)(2,1)S(1)} %get-tuple-element.29.ug), custom_call_target="tpu_custom_call" | custom-call | flops 524288000 | tf_op jit(solution)/shard_map/pallas_call | solution.py:305
  127.3 0.0 collective-permute-done.3.far
  127.3 4.4 %all-to-all-done.4.ret = bf16[128,8,128]{2,1,0:T(8,128)(2,1)S(1)} async-done(((bf16[128,8,128]{2,1,0:T(8,128)(2,1)}), bf16[128,8,128]{2,1,0:T(8,128)(2,1)S(1)}, u32[]{:S(2)}, u32[]{:S(2)}) %all-to-all-start.4) | async-done | bytes 262176 | tf_op jit(solution)/shard_map/all_to_all | solution.py:380
  131.6 1.1 shard_map.110
  (7 shorter events, 0.1 us)
Async XLA Ops:
  2.5 18.9 %copy-start.6 = (bf16[32,16,128]{2,1,0:T(8,128)(2,1)S(1)}, bf16[32,16,128]{2,1,0:T(8,128)(2,1)}, u32[]{:S(2)}) copy-start(bf16[32,16,128]{2,1,0:T(8,128)(2,1)} %get-tuple-element.17) | copy-start | bytes 393220
  2.5 39.9 %copy-start.4 = (bf16[8,128]{1,0:T(8,128)(2,1)S(1)}, bf16[8,128]{1,0:T(8,128)(2,1)}, u32[]{:S(2)}) copy-start(bf16[8,128]{1,0:T(8,128)(2,1)} %get-tuple-element.18.tile_h.tile) | copy-start | bytes 6148
  5.4 37.0 %collective-permute-start = (bf16[496,2048]{1,0:T(8,128)(2,1)}, bf16[496,2048]{1,0:T(8,128)(2,1)S(1)}, u32[]{:S(2)}, u32[]{:S(2)}) collective-permute-start(bf16[496,2048]{1,0:T(8,128)(2,1)} %shard_map.104.mine), channel_id=1, source_target_pairs={{0,32},{32,0},{1,33},{33,1},{2,34},{34,2},{3,35},{35,3},{4,36},{36... | collective-permute-start | bytes 6094856 | tf_op jit(solution)/shard_map/ppermute | solution.py:361
  57.8 19.7 %copy-start = (bf16[496,2048]{1,0:T(8,128)(2,1)S(1)}, bf16[496,2048]{1,0:T(8,128)(2,1)}, u32[]{:S(2)}) copy-start(bf16[496,2048]{1,0:T(8,128)(2,1)} %shard_map.104.mine) | copy-start | bytes 6094852
  57.8 19.7 %copy-start.1 = (bf16[256,64]{0,1:T(8,128)(2,1)S(1)}, bf16[256,64]{0,1:T(8,128)(2,1)}, u32[]{:S(2)}) copy-start(bf16[256,64]{0,1:T(8,128)(2,1)} %param.8) | copy-start | bytes 98308
  57.8 19.7 %copy-start.2 = (f32[256,32]{0,1:T(8,128)S(1)}, f32[256,32]{0,1:T(8,128)}, u32[]{:S(2)}) copy-start(f32[256,32]{0,1:T(8,128)} %param.11) | copy-start | bytes 98308
  57.8 19.7 %copy-start.3 = (s32[256,1]{0,1:T(1,128)S(1)}, s32[256,1]{0,1:T(1,128)}, u32[]{:S(2)}) copy-start(s32[256,1]{0,1:T(1,128)} %param.12) | copy-start | bytes 3076
  91.2 20.5 %collective-permute-start.1 = (bf16[192,2560]{1,0:T(8,128)(2,1)S(1)}, bf16[192,2560]{1,0:T(8,128)(2,1)S(1)}, u32[]{:S(2)}, u32[]{:S(2)}) collective-permute-start(bf16[192,2560]{1,0:T(8,128)(2,1)S(1)} %get-tuple-element.26.mine), channel_id=1, source_target_pairs={{0,32},{32,0},{1,33},{33,1},{2,34},{34,2},{3,35},{35,3},{4,36},{36... | collective-permute-start | bytes 2949128 | tf_op jit(solution)/shard_map/ppermute | solution.py:381
  97.8 33.9 %all-to-all-start.4 = ((bf16[128,8,128]{2,1,0:T(8,128)(2,1)}), bf16[128,8,128]{2,1,0:T(8,128)(2,1)S(1)}, u32[]{:S(2)}, u32[]{:S(2)}) async-start(bf16[128,8,128]{2,1,0:T(8,128)(2,1)} %get-tuple-element.23), calls=%async_computation.4 | async-start | bytes 524288 | tf_op jit(solution)/shard_map/all_to_all | solution.py:380
  111.8 8.2 %collective-permute-start.2 = (bf16[32,128]{1,0:T(8,128)(2,1)S(1)}, bf16[32,128]{1,0:T(8,128)(2,1)S(1)}, u32[]{:S(2)}, u32[]{:S(2)}) collective-permute-start(bf16[32,128]{1,0:T(8,128)(2,1)S(1)} %shard_map.108.a), channel_id=1, source_target_pairs={{0,256},{256,0},{512,768},{768,512},{1,257},{257,1},{513,769},{769... | collective-permute-start | bytes 24584 | tf_op jit(solution)/shard_map/ppermute | solution.py:383
  120.1 7.2 %collective-permute-start.3 = (bf16[32,128]{1,0:T(8,128)(2,1)S(1)}, bf16[32,128]{1,0:T(8,128)(2,1)S(1)}, u32[]{:S(2)}, u32[]{:S(2)}) collective-permute-start(bf16[32,128]{1,0:T(8,128)(2,1)S(1)} %shard_map.109.pair), channel_id=1, source_target_pairs={{0,512},{512,0},{256,768},{768,256},{1,513},{513,1},{257,769},{769... | collective-permute-start | bytes 24584 | tf_op jit(solution)/shard_map/ppermute | solution.py:386
  125.3 6.3 %copy-start.5 = (bf16[64,32]{0,1:T(8,128)(2,1)S(1)}, bf16[64,32]{0,1:T(8,128)(2,1)}, u32[]{:S(2)}) copy-start(bf16[64,32]{0,1:T(8,128)(2,1)} %param.15) | copy-start | bytes 12292

commit v5 on v4

--- a/solution.py
+++ b/solution.py
@@ -25,7 +25,13 @@
 HID = 160
 BUNDLE = 3 * HID + 16
 WIDE = D + 512
-FROM_LAST = list(range(E))[::-1]
+AWAY = [4 * y + z for y in (7, 6, 5, 4, 0, 1, 2, 3) for z in (3, 2, 0, 1)]
+NEAR = [1, 0, 2, 3]
+HOME = [
+    E * (z % 4) + 4 * (y % 8) + z % 16 // 4
+    for z in (*range(0, -8, -1), *range(1, 9))
+    for y in (0, -1, -2, -3, 1, 2, 3, 4)
+]
 DISPATCH_KIB = 60000
 CROSS = GROUPS * CAP + E
 F32, BF16 = jnp.float32, jnp.bfloat16
@@ -68,8 +74,10 @@
     idx = ix[...]
     hot, slot = slots(idx)
     row = iota((E * 16, T), 0)
+    y, z = lax.shift_right_logical(row, 6), lax.bitwise_and(lax.shift_right_logical(row, 4), 3)
+    expert = 4 * jnp.where(y < 4, 7 - y, y - 4) + jnp.where(z < 2, 3 - z, z - 2)
     sel = jnp.where(
-        (E - 1 - lax.shift_right_logical(row, 4) == idx)
+        (expert == idx)
         & (lax.bitwise_and(row, 15) == slot.astype(jnp.int32)),
         1.0,
         0.0,
@@ -123,8 +131,8 @@
     tail = [jnp.zeros((8, 128), F32) for _ in range(KT // 4)]
     total = jnp.zeros((16, 128), F32)
     for j in range(E // 2):
-        a = got[E - 1 - 2 * j].astype(F32)
-        b = got[E - 2 - 2 * j].astype(F32)
+        a = got[AWAY.index(2 * j)].astype(F32)
+        b = got[AWAY.index(2 * j + 1)].astype(F32)
         total = total + a + b
         t = jnp.where(low, a, pltpu.roll(b, F, 1))
         g = jnp.where(low, pltpu.roll(a, F, 1), b)
@@ -244,8 +252,8 @@
                 head = total(k)
                 rest = tail if i == 0 else pltpu.roll(tail, 8 - 2 * i, 0)
                 rest = jnp.where(line < 2, rest, 0.0)
-                out[E * z + 2 * k] = jnp.where(low, head, pltpu.roll(rest, F, 1)).astype(BF16)
-                out[E * z + 2 * k + 1] = jnp.where(low, pltpu.roll(head, F, 1), rest).astype(BF16)
+                out[HOME.index(E * NEAR[z] + 2 * k)] = jnp.where(low, head, pltpu.roll(rest, F, 1)).astype(BF16)
+                out[HOME.index(E * NEAR[z] + 2 * k + 1)] = jnp.where(low, pltpu.roll(head, F, 1), rest).astype(BF16)
     share = merged(got, ZL * BACK)
     share_ref[...] = share
     bundle[: GROUPS * CAP, :] = cross[...]
@@ -285,17 +293,16 @@
     row = iota((E * 8, T), 0)
     mine = lax.shift_right_logical(row, 3) == idx
     c = lax.bitwise_and(row, 7)
-    r = ret[pl.ds(0, E)].astype(F32)
-    for z in range(1, ZL):
-        r = r + ret[pl.ds(E * z, E)].astype(F32)
+    r = jnp.concatenate(
+        [sum(ret[HOME.index(E * z + e)].astype(F32) for z in range(ZL)) for e in range(E)], axis=0
+    )
     high = r.astype(BF16)
     low = (r - high.astype(F32)).astype(BF16)
     acc = lax.dot_general(rw[...], lg[...], CONTRACT_FIRST, preferred_element_type=F32)
     for h in range(2):
         sel = jnp.where(mine & (c + 8 * h == slot), 1.0, 0.0).astype(BF16)
         for part in (high, low):
-            lanes = part.reshape(E * 8, 128)
-            p = lax.dot_general(lanes, sel, CONTRACT_FIRST, preferred_element_type=F32)
+            p = lax.dot_general(part, sel, CONTRACT_FIRST, preferred_element_type=F32)
             acc = acc + p[F * h : F * (h + 1)]
     out[...] = acc.astype(BF16)
 
@@ -348,7 +355,7 @@
         hbm=True,
         kib=DISPATCH_KIB,
     )
-    got = lax.all_to_all(send, EX, 0, 0, tiled=True, axis_index_groups=[FROM_LAST])
+    got = lax.all_to_all(send, EX, 0, 0, tiled=True, axis_index_groups=[AWAY])
     mine = local(
         bundle_kernel,
         shape(BUNDLE, D),
@@ -360,8 +367,8 @@
     )
     other = lax.ppermute(mine, "core", swap)
     packed, gate_dot = local(pack_kernel, (shape(SENT, 8, 128), shape(1, T, dtype=F32)), (got, tile, other), 10**7)
-    line = lax.all_to_all(jnp.broadcast_to(packed, (ZL, *packed.shape)), "zl", 0, 0, tiled=True)
-    plane = lax.all_to_all(jnp.broadcast_to(line, (X, *line.shape)), "x", 0, 0, tiled=True)
+    line = lax.all_to_all(jnp.broadcast_to(packed, (ZL, *packed.shape)), "zl", 0, 0, tiled=True, axis_index_groups=[NEAR])
+    plane = lax.all_to_all(jnp.broadcast_to(line, (X, *line.shape)), "x", 0, 0, tiled=True, axis_index_groups=[NEAR])
     own = plane.reshape(GROUPS, SENT, 8, 128)
     rows = GROUPS * CAP
     work = 10 * rows * HID * D
@@ -373,11 +380,11 @@
         (pltpu.VMEM((rows, D), BF16),),
         kib=20000,
     )
-    landed = lax.all_to_all(back, "x", 0, 0, tiled=True)
+    landed = lax.all_to_all(back, "x", 0, 0, tiled=True, axis_index_groups=[NEAR])
     rows_back, bundle, share = local(
         middle_kernel, (shape(ZL * E, 8, 128), shape(CROSS, WIDE), shape(E, 128, dtype=F32)), (landed, cross), 10**6
     )
-    ret = lax.all_to_all(rows_back, ("zl", EX), 0, 0, tiled=True)
+    ret = lax.all_to_all(rows_back, ("zl", EX), 0, 0, tiled=True, axis_index_groups=[HOME])
     came = lax.ppermute(bundle, "core", swap)
     pair = local(cores_kernel, shape(E, 128), (share, came), 10**5)
     got = lax.ppermute(pair, "zl", [(0, 1), (1, 0), (2, 3), (3, 2)])

time: 135 us -> 134 us (level)
  waiting for transfers between devices: 10 us -> 12.4 us
  starting transfers between devices: 44.3 us -> 42 us
    all_to_all x1, starting transfers between devices: 13.9 us -> 11.3 us  [layer(): lax.all_to_all(rows_back, ('zl', EX), 0, 0, tiled=True, axis_index_groups...]
    all_to_all x1, waiting for transfers between devices: 4.37 us -> 5.95 us  [layer(): lax.all_to_all(rows_back, ('zl', EX), 0, 0, tiled=True, axis_index_groups...]
where the time goes in v5:
time: 134 us; the launch traced here: 132 us
  blocking collectives  65.2 us (49%)
  starting transfers between devices  42 us (31%)
  waiting for transfers between devices  12.4 us (9%)
  Pallas kernels  11.5 us (9%)
    all_to_all x1, blocking collectives, layer(): got = lax.all_to_all(send, EX, 0, 0, tiled=True, axis_index_groups=[AWAY])  21.2 us
    all_to_all x1, blocking collectives, layer(): lax.all_to_all(jnp.broadcast_to(line, (X, *line.shape)), 'x', 0, 0, tiled...  18.6 us
    ppermute x1, starting transfers between devices, layer(): other = lax.ppermute(mine, 'core', swap)  16 us
    all_to_all x1, blocking collectives, layer(): lax.all_to_all(jnp.broadcast_to(packed, (ZL, *packed.shape)), 'zl', 0, 0,...  15.1 us
    pallas_call x9, Pallas kernels, local(): pl.pallas_call(kernel, out_shape=outs, in_specs=[pl.BlockSpec(memory_spac...  11.5 us
    all_to_all x1, starting transfers between devices, layer(): lax.all_to_all(rows_back, ('zl', EX), 0, 0, tiled=True, axis_index_groups...  11.3 us
    all_to_all x1, blocking collectives, layer(): lax.all_to_all(back, 'x', 0, 0, tiled=True, axis_index_groups=[NEAR])  10.4 us
    ppermute x1, starting transfers between devices, layer(): came = lax.ppermute(bundle, 'core', swap)  6.86 us
  transfers between devices with their start and end apart: 5, of which 2 were waited for; matrix products, arithmetic and copies ran while one was open for 0% of the time, Pallas kernels for 2%

profile of v5, /device:TPU:1, one launch (start us, length us, event | category | flops | bytes accessed | tf_op | source)
XLA Modules:
  0.0 132.1 jit_solution(18224647929165571116)
XLA Ops:
  0.6 1.9 %shard_map.103 = (bf16[32,16,128]{2,1,0:T(8,128)(2,1)}, bf16[8,128]{1,0:T(8,128)(2,1)}) custom-call(bf16[64,256]{1,0:T(8,128)(2,1)} %bitcast.13, bf16[64,256]{1,0:T(8,128)(2,1)} %bitcast.24, bf16[64,256]{1,0:T(8,128)(2,1)} %bitcast.25, f32[32,256]{1,0:T(8,128)} %bitcast.15, s32[1,256]{1,0:T(1,128)} %bitcast.17), custom_call_target="tpu_custom_call" | custom-call | flops 10000000 | tf_op jit(solution)/shard_map/pallas_call | solution.py:312
  2.5 0.0 copy-start.6
  2.5 0.0 copy-start.4
  2.5 2.9 %shard_map.104.mine = bf16[496,2048]{1,0:T(8,128)(2,1)} custom-call(bf16[2,160,2048]{2,1,0:T(8,128)(2,1)} %bitcast.21, bf16[160,2048]{1,0:T(8,128)(2,1)} %bitcast.23, bf16[8,128]{1,0:T(8,128)(2,1)} %get-tuple-element.18.tile_h.tile), custom_call_target="tpu_custom_call" | custom-call | flops 1000000 | tf_op jit(solution)/shard_map/pallas_call | solution.py:312
  5.4 16.0 %collective-permute-start = (bf16[496,2048]{1,0:T(8,128)(2,1)}, bf16[496,2048]{1,0:T(8,128)(2,1)S(1)}, u32[]{:S(2)}, u32[]{:S(2)}) collective-permute-start(bf16[496,2048]{1,0:T(8,128)(2,1)} %shard_map.104.mine), channel_id=1, source_target_pairs={{0,32},{32,0},{1,33},{33,1},{2,34},{34,2},{3,35},{35,3},{4,36},{36... | collective-permute-start | bytes 6094856 | tf_op jit(solution)/shard_map/ppermute | solution.py:368
  21.5 0.0 copy-done.6
  21.5 21.2 %all_to_all.25.got = bf16[32,16,128]{2,1,0:T(8,128)(2,1)S(1)} all-to-all(bf16[32,16,128]{2,1,0:T(8,128)(2,1)S(1)} %copy-done.6), channel_id=1, replica_groups={{31,30,28,29,27,26,24,25,23,22,20,21,19,18,16,17,3,2,0,1,7,6,4,5,11,10,..., dimensions={0} | all-to-all | bytes 262144 | tf_op jit(solution)/shard_map/all_to_all | solution.py:358
  42.7 0.0 collective-permute-done.partner.other
  42.7 0.1 shard_map.105
  42.8 15.1 %all_to_all.26 = bf16[4,41,8,128]{3,2,1,0:T(8,128)(2,1)S(1)} all-to-all(bf16[4,41,8,128]{3,2,1,0:T(8,128)(2,1)S(1)} %broadcast_in_dim.9), channel_id=1, replica_groups={{256,0,512,768},{257,1,513,769},{258,2,514,770},{259,3,515,771},{260,4,..., dimensions={0} | all-to-all | bytes 671744 | tf_op jit(solution)/shard_map/all_to_all | solution.py:370
  57.9 0.2 broadcast_in_dim.10
  58.1 0.0 copy-start.1
  58.1 0.0 copy-start.2
  58.1 0.0 copy-start.3
  58.1 18.6 %all_to_all.27 = bf16[4,4,41,8,128]{4,3,2,1,0:T(8,128)(2,1)S(1)} all-to-all(bf16[4,4,41,8,128]{4,3,2,1,0:T(8,128)(2,1)S(1)} %broadcast_in_dim.10), channel_id=1, replica_groups={{64,0,128,192},{65,1,129,193},{66,2,130,194},{67,3,131,195},{68,4,132,1..., dimensions={0} | all-to-all | bytes 2686976 | tf_op jit(solution)/shard_map/all_to_all | solution.py:371
  76.7 0.0 copy-done.1
  76.7 2.6 %shard_map.106 = (bf16[4,84,8,128]{3,2,1,0:T(8,128)(2,1)S(1)}, bf16[160,2560]{1,0:T(8,128)(2,1)S(1)}, bf16[160,160]{1,0:T(8,128)(2,1)S(1)}, bf16[160,160]{1,0:T(8,128)(2,1)S(1)}, bf16[32,256]{1,0:T(8,128)(2,1)S(1)}) custom-call(bf16[16,41,8,128]{3,2,1,0:T(8,128)(2,1)S(1)} %bitcast.12, bf16[496,2048]{1,0:T(8,128)(2,1)S(1)} %copy-done, ...), custom_call_target="tpu_custom_call" | custom-call | flops 1048576000 | tf_op jit(solution)/shard_map/pallas_call | solution.py:312
  79.3 10.4 %all_to_all.28.got = bf16[4,84,8,128]{3,2,1,0:T(8,128)(2,1)S(1)} all-to-all(bf16[4,84,8,128]{3,2,1,0:T(8,128)(2,1)S(1)} %get-tuple-element.21), channel_id=1, replica_groups={{64,0,128,192},{65,1,129,193},{66,2,130,194},{67,3,131,195},{68,4,132,1..., dimensions={0} | all-to-all | bytes 1376256 | tf_op jit(solution)/shard_map/all_to_all | solution.py:383
  89.7 0.9 shard_map.107
  90.6 6.9 %collective-permute-start.1 = (bf16[192,2560]{1,0:T(8,128)(2,1)S(1)}, bf16[192,2560]{1,0:T(8,128)(2,1)S(1)}, u32[]{:S(2)}, u32[]{:S(2)}) collective-permute-start(bf16[192,2560]{1,0:T(8,128)(2,1)S(1)} %get-tuple-element.26.mine), channel_id=1, source_target_pairs={{0,32},{32,0},{1,33},{33,1},{2,34},{34,2},{3,35},{35,3},{4,36},{36... | collective-permute-start | bytes 2949128 | tf_op jit(solution)/shard_map/ppermute | solution.py:388
  97.5 11.3 %all-to-all-start.4 = ((bf16[128,8,128]{2,1,0:T(8,128)(2,1)}), bf16[128,8,128]{2,1,0:T(8,128)(2,1)S(1)}, u32[]{:S(2)}, u32[]{:S(2)}) async-start(bf16[128,8,128]{2,1,0:T(8,128)(2,1)} %get-tuple-element.23), calls=%async_computation.4 | async-start | bytes 524288 | tf_op jit(solution)/shard_map/all_to_all | solution.py:387
  108.8 0.0 collective-permute-done.1.came
  108.8 0.1 shard_map.108.a
  108.9 2.8 %collective-permute-start.2 = (bf16[32,128]{1,0:T(8,128)(2,1)S(1)}, bf16[32,128]{1,0:T(8,128)(2,1)S(1)}, u32[]{:S(2)}, u32[]{:S(2)}) collective-permute-start(bf16[32,128]{1,0:T(8,128)(2,1)S(1)} %shard_map.108.a), channel_id=1, source_target_pairs={{0,256},{256,0},{512,768},{768,512},{1,257},{257,1},{513,769},{769... | collective-permute-start | bytes 24584 | tf_op jit(solution)/shard_map/ppermute | solution.py:390
  111.7 6.4 %collective-permute-done.2.b = bf16[32,128]{1,0:T(8,128)(2,1)S(1)} collective-permute-done((bf16[32,128]{1,0:T(8,128)(2,1)S(1)}, bf16[32,128]{1,0:T(8,128)(2,1)S(1)}, u32[]{:S(2)}, u32[]{:S(2)}) %collective-permute-start.2) | collective-permute-done | bytes 8224 | tf_op jit(solution)/shard_map/ppermute | solution.py:390
  118.1 0.1 shard_map.109.pair
  118.1 5.0 %collective-permute-start.3 = (bf16[32,128]{1,0:T(8,128)(2,1)S(1)}, bf16[32,128]{1,0:T(8,128)(2,1)S(1)}, u32[]{:S(2)}, u32[]{:S(2)}) collective-permute-start(bf16[32,128]{1,0:T(8,128)(2,1)S(1)} %shard_map.109.pair), channel_id=1, source_target_pairs={{0,512},{512,0},{256,768},{768,256},{1,513},{513,1},{257,769},{769... | collective-permute-start | bytes 24584 | tf_op jit(solution)/shard_map/ppermute | solution.py:393
  123.2 0.0 copy-start.5
  123.2 1.9 %shard_map.111 = bf16[2,160,2048]{2,1,0:T(8,128)(2,1)} custom-call(bf16[192,2560]{1,0:T(8,128)(2,1)S(1)} %get-tuple-element.26.mine, bf16[192,2560]{1,0:T(8,128)(2,1)S(1)} %collective-permute-done.1.came, bf16[160,160]{1,0:T(8,128)(2,1)S(1)} %get-tuple-element.28.gg, bf16[160,160]{1,0:T(8,128)(2,1)S(1)} %get-tuple-element.29.ug), custom_call_target="tpu_custom_call" | custom-call | flops 524288000 | tf_op jit(solution)/shard_map/pallas_call | solution.py:312
  125.1 0.0 collective-permute-done.3.far
  125.1 6.0 %all-to-all-done.4.ret = bf16[128,8,128]{2,1,0:T(8,128)(2,1)S(1)} async-done(((bf16[128,8,128]{2,1,0:T(8,128)(2,1)}), bf16[128,8,128]{2,1,0:T(8,128)(2,1)S(1)}, u32[]{:S(2)}, u32[]{:S(2)}) %all-to-all-start.4) | async-done | bytes 262176 | tf_op jit(solution)/shard_map/all_to_all | solution.py:387
  131.1 1.1 shard_map.110
  (7 shorter events, 0.1 us)
Async XLA Ops:
  2.5 18.9 %copy-start.6 = (bf16[32,16,128]{2,1,0:T(8,128)(2,1)S(1)}, bf16[32,16,128]{2,1,0:T(8,128)(2,1)}, u32[]{:S(2)}) copy-start(bf16[32,16,128]{2,1,0:T(8,128)(2,1)} %get-tuple-element.17) | copy-start | bytes 393220
  2.5 40.1 %copy-start.4 = (bf16[8,128]{1,0:T(8,128)(2,1)S(1)}, bf16[8,128]{1,0:T(8,128)(2,1)}, u32[]{:S(2)}) copy-start(bf16[8,128]{1,0:T(8,128)(2,1)} %get-tuple-element.18.tile_h.tile) | copy-start | bytes 6148
  5.4 37.2 %collective-permute-start = (bf16[496,2048]{1,0:T(8,128)(2,1)}, bf16[496,2048]{1,0:T(8,128)(2,1)S(1)}, u32[]{:S(2)}, u32[]{:S(2)}) collective-permute-start(bf16[496,2048]{1,0:T(8,128)(2,1)} %shard_map.104.mine), channel_id=1, source_target_pairs={{0,32},{32,0},{1,33},{33,1},{2,34},{34,2},{3,35},{35,3},{4,36},{36... | collective-permute-start | bytes 6094856 | tf_op jit(solution)/shard_map/ppermute | solution.py:368
  58.1 18.6 %copy-start = (bf16[496,2048]{1,0:T(8,128)(2,1)S(1)}, bf16[496,2048]{1,0:T(8,128)(2,1)}, u32[]{:S(2)}) copy-start(bf16[496,2048]{1,0:T(8,128)(2,1)} %shard_map.104.mine) | copy-start | bytes 6094852
  58.1 18.6 %copy-start.1 = (bf16[256,64]{0,1:T(8,128)(2,1)S(1)}, bf16[256,64]{0,1:T(8,128)(2,1)}, u32[]{:S(2)}) copy-start(bf16[256,64]{0,1:T(8,128)(2,1)} %param.8) | copy-start | bytes 98308
  58.1 18.6 %copy-start.2 = (f32[256,32]{0,1:T(8,128)S(1)}, f32[256,32]{0,1:T(8,128)}, u32[]{:S(2)}) copy-start(f32[256,32]{0,1:T(8,128)} %param.11) | copy-start | bytes 98308
  58.1 18.6 %copy-start.3 = (s32[256,1]{0,1:T(1,128)S(1)}, s32[256,1]{0,1:T(1,128)}, u32[]{:S(2)}) copy-start(s32[256,1]{0,1:T(1,128)} %param.12) | copy-start | bytes 3076
  90.6 18.2 %collective-permute-start.1 = (bf16[192,2560]{1,0:T(8,128)(2,1)S(1)}, bf16[192,2560]{1,0:T(8,128)(2,1)S(1)}, u32[]{:S(2)}, u32[]{:S(2)}) collective-permute-start(bf16[192,2560]{1,0:T(8,128)(2,1)S(1)} %get-tuple-element.26.mine), channel_id=1, source_target_pairs={{0,32},{32,0},{1,33},{33,1},{2,34},{34,2},{3,35},{35,3},{4,36},{36... | collective-permute-start | bytes 2949128 | tf_op jit(solution)/shard_map/ppermute | solution.py:388
  97.5 33.6 %all-to-all-start.4 = ((bf16[128,8,128]{2,1,0:T(8,128)(2,1)}), bf16[128,8,128]{2,1,0:T(8,128)(2,1)S(1)}, u32[]{:S(2)}, u32[]{:S(2)}) async-start(bf16[128,8,128]{2,1,0:T(8,128)(2,1)} %get-tuple-element.23), calls=%async_computation.4 | async-start | bytes 524288 | tf_op jit(solution)/shard_map/all_to_all | solution.py:387
  108.9 9.2 %collective-permute-start.2 = (bf16[32,128]{1,0:T(8,128)(2,1)S(1)}, bf16[32,128]{1,0:T(8,128)(2,1)S(1)}, u32[]{:S(2)}, u32[]{:S(2)}) collective-permute-start(bf16[32,128]{1,0:T(8,128)(2,1)S(1)} %shard_map.108.a), channel_id=1, source_target_pairs={{0,256},{256,0},{512,768},{768,512},{1,257},{257,1},{513,769},{769... | collective-permute-start | bytes 24584 | tf_op jit(solution)/shard_map/ppermute | solution.py:390
  118.1 7.0 %collective-permute-start.3 = (bf16[32,128]{1,0:T(8,128)(2,1)S(1)}, bf16[32,128]{1,0:T(8,128)(2,1)S(1)}, u32[]{:S(2)}, u32[]{:S(2)}) collective-permute-start(bf16[32,128]{1,0:T(8,128)(2,1)S(1)} %shard_map.109.pair), channel_id=1, source_target_pairs={{0,512},{512,0},{256,768},{768,256},{1,513},{513,1},{257,769},{769... | collective-permute-start | bytes 24584 | tf_op jit(solution)/shard_map/ppermute | solution.py:393
  123.2 7.9 %copy-start.5 = (bf16[64,32]{0,1:T(8,128)(2,1)S(1)}, bf16[64,32]{0,1:T(8,128)(2,1)}, u32[]{:S(2)}) copy-start(bf16[64,32]{0,1:T(8,128)(2,1)} %param.15) | copy-start | bytes 12292

commit v6 on v5

--- a/solution.py
+++ b/solution.py
@@ -28,9 +28,11 @@
 AWAY = [4 * y + z for y in (7, 6, 5, 4, 0, 1, 2, 3) for z in (3, 2, 0, 1)]
 NEAR = [1, 0, 2, 3]
 HOME = [
-    E * (z % 4) + 4 * (y % 8) + z % 16 // 4
-    for z in (*range(0, -8, -1), *range(1, 9))
-    for y in (0, -1, -2, -3, 1, 2, 3, 4)
+    E * z + 4 * (4 * far + y) + zh
+    for zh in (0, 3, 1, 2)
+    for far in (0, 1)
+    for z in NEAR
+    for y in NEAR
 ]
 DISPATCH_KIB = 60000
 CROSS = GROUPS * CAP + E

time: 134 us -> 135 us (level)
  waiting for transfers between devices: 12.4 us -> 15.2 us
  starting transfers between devices: 42 us -> 40.6 us
    all_to_all x1, waiting for transfers between devices: 5.95 us -> 8.31 us  [layer(): lax.all_to_all(rows_back, ('zl', EX), 0, 0, tiled=True, axis_index_groups...]
  transfers between devices with their start and end apart: 5 -> 5, of which waited for: 2 -> 3; matrix products, arithmetic and copies ran while one was open for 0% -> 0% of each run, Pallas kernels for 2% -> 2%
where the time goes in v6:
time: 135 us; the launch traced here: 134 us
  blocking collectives  65.2 us (48%)
  starting transfers between devices  40.6 us (30%)
  waiting for transfers between devices  15.2 us (11%)
  Pallas kernels  11.5 us (9%)
    all_to_all x1, blocking collectives, layer(): got = lax.all_to_all(send, EX, 0, 0, tiled=True, axis_index_groups=[AWAY])  21.2 us
    all_to_all x1, blocking collectives, layer(): lax.all_to_all(jnp.broadcast_to(line, (X, *line.shape)), 'x', 0, 0, tiled...  18.6 us
    ppermute x1, starting transfers between devices, layer(): other = lax.ppermute(mine, 'core', swap)  16 us
    all_to_all x1, blocking collectives, layer(): lax.all_to_all(jnp.broadcast_to(packed, (ZL, *packed.shape)), 'zl', 0, 0,...  15.1 us
    all_to_all x1, starting transfers between devices, layer(): lax.all_to_all(rows_back, ('zl', EX), 0, 0, tiled=True, axis_index_groups...  11.9 us
    pallas_call x9, Pallas kernels, local(): pl.pallas_call(kernel, out_shape=outs, in_specs=[pl.BlockSpec(memory_spac...  11.5 us
    all_to_all x1, blocking collectives, layer(): lax.all_to_all(back, 'x', 0, 0, tiled=True, axis_index_groups=[NEAR])  10.4 us
    all_to_all x1, waiting for transfers between devices, layer(): lax.all_to_all(rows_back, ('zl', EX), 0, 0, tiled=True, axis_index_groups...  8.31 us
  transfers between devices with their start and end apart: 5, of which 3 were waited for; matrix products, arithmetic and copies ran while one was open for 0% of the time, Pallas kernels for 2%

profile of v6, /device:TPU:1, one launch (start us, length us, event | category | flops | bytes accessed | tf_op | source)
XLA Modules:
  0.0 133.6 jit_solution(2360575809102043808)
XLA Ops:
  0.6 1.9 %shard_map.103 = (bf16[32,16,128]{2,1,0:T(8,128)(2,1)}, bf16[8,128]{1,0:T(8,128)(2,1)}) custom-call(bf16[64,256]{1,0:T(8,128)(2,1)} %bitcast.13, bf16[64,256]{1,0:T(8,128)(2,1)} %bitcast.24, bf16[64,256]{1,0:T(8,128)(2,1)} %bitcast.25, f32[32,256]{1,0:T(8,128)} %bitcast.15, s32[1,256]{1,0:T(1,128)} %bitcast.17), custom_call_target="tpu_custom_call" | custom-call | flops 10000000 | tf_op jit(solution)/shard_map/pallas_call | solution.py:314
  2.5 0.0 copy-start.6
  2.5 0.0 copy-start.4
  2.5 2.9 %shard_map.104.mine = bf16[496,2048]{1,0:T(8,128)(2,1)} custom-call(bf16[2,160,2048]{2,1,0:T(8,128)(2,1)} %bitcast.21, bf16[160,2048]{1,0:T(8,128)(2,1)} %bitcast.23, bf16[8,128]{1,0:T(8,128)(2,1)} %get-tuple-element.18.tile_h.tile), custom_call_target="tpu_custom_call" | custom-call | flops 1000000 | tf_op jit(solution)/shard_map/pallas_call | solution.py:314
  5.4 16.0 %collective-permute-start = (bf16[496,2048]{1,0:T(8,128)(2,1)}, bf16[496,2048]{1,0:T(8,128)(2,1)S(1)}, u32[]{:S(2)}, u32[]{:S(2)}) collective-permute-start(bf16[496,2048]{1,0:T(8,128)(2,1)} %shard_map.104.mine), channel_id=1, source_target_pairs={{0,32},{32,0},{1,33},{33,1},{2,34},{34,2},{3,35},{35,3},{4,36},{36... | collective-permute-start | bytes 6094856 | tf_op jit(solution)/shard_map/ppermute | solution.py:370
  21.5 0.0 copy-done.6
  21.5 21.2 %all_to_all.25.got = bf16[32,16,128]{2,1,0:T(8,128)(2,1)S(1)} all-to-all(bf16[32,16,128]{2,1,0:T(8,128)(2,1)S(1)} %copy-done.6), channel_id=1, replica_groups={{31,30,28,29,27,26,24,25,23,22,20,21,19,18,16,17,3,2,0,1,7,6,4,5,11,10,..., dimensions={0} | all-to-all | bytes 262144 | tf_op jit(solution)/shard_map/all_to_all | solution.py:360
  42.7 0.0 collective-permute-done.partner.other
  42.7 0.1 shard_map.105
  42.8 15.1 %all_to_all.26 = bf16[4,41,8,128]{3,2,1,0:T(8,128)(2,1)S(1)} all-to-all(bf16[4,41,8,128]{3,2,1,0:T(8,128)(2,1)S(1)} %broadcast_in_dim.9), channel_id=1, replica_groups={{256,0,512,768},{257,1,513,769},{258,2,514,770},{259,3,515,771},{260,4,..., dimensions={0} | all-to-all | bytes 671744 | tf_op jit(solution)/shard_map/all_to_all | solution.py:372
  57.9 0.2 broadcast_in_dim.10
  58.1 0.0 copy-start.1
  58.1 0.0 copy-start.2
  58.1 0.0 copy-start.3
  58.1 18.6 %all_to_all.27 = bf16[4,4,41,8,128]{4,3,2,1,0:T(8,128)(2,1)S(1)} all-to-all(bf16[4,4,41,8,128]{4,3,2,1,0:T(8,128)(2,1)S(1)} %broadcast_in_dim.10), channel_id=1, replica_groups={{64,0,128,192},{65,1,129,193},{66,2,130,194},{67,3,131,195},{68,4,132,1..., dimensions={0} | all-to-all | bytes 2686976 | tf_op jit(solution)/shard_map/all_to_all | solution.py:373
  76.7 0.0 copy-done.1
  76.7 2.6 %shard_map.106 = (bf16[4,84,8,128]{3,2,1,0:T(8,128)(2,1)S(1)}, bf16[160,2560]{1,0:T(8,128)(2,1)S(1)}, bf16[160,160]{1,0:T(8,128)(2,1)S(1)}, bf16[160,160]{1,0:T(8,128)(2,1)S(1)}, bf16[32,256]{1,0:T(8,128)(2,1)S(1)}) custom-call(bf16[16,41,8,128]{3,2,1,0:T(8,128)(2,1)S(1)} %bitcast.12, bf16[496,2048]{1,0:T(8,128)(2,1)S(1)} %copy-done, ...), custom_call_target="tpu_custom_call" | custom-call | flops 1048576000 | tf_op jit(solution)/shard_map/pallas_call | solution.py:314
  79.3 10.4 %all_to_all.28.got = bf16[4,84,8,128]{3,2,1,0:T(8,128)(2,1)S(1)} all-to-all(bf16[4,84,8,128]{3,2,1,0:T(8,128)(2,1)S(1)} %get-tuple-element.21), channel_id=1, replica_groups={{64,0,128,192},{65,1,129,193},{66,2,130,194},{67,3,131,195},{68,4,132,1..., dimensions={0} | all-to-all | bytes 1376256 | tf_op jit(solution)/shard_map/all_to_all | solution.py:385
  89.7 0.9 shard_map.107
  90.6 6.9 %collective-permute-start.1 = (bf16[192,2560]{1,0:T(8,128)(2,1)S(1)}, bf16[192,2560]{1,0:T(8,128)(2,1)S(1)}, u32[]{:S(2)}, u32[]{:S(2)}) collective-permute-start(bf16[192,2560]{1,0:T(8,128)(2,1)S(1)} %get-tuple-element.26.mine), channel_id=1, source_target_pairs={{0,32},{32,0},{1,33},{33,1},{2,34},{34,2},{3,35},{35,3},{4,36},{36... | collective-permute-start | bytes 2949128 | tf_op jit(solution)/shard_map/ppermute | solution.py:390
  97.5 11.9 %all-to-all-start.4 = ((bf16[128,8,128]{2,1,0:T(8,128)(2,1)}), bf16[128,8,128]{2,1,0:T(8,128)(2,1)S(1)}, u32[]{:S(2)}, u32[]{:S(2)}) async-start(bf16[128,8,128]{2,1,0:T(8,128)(2,1)} %get-tuple-element.23), calls=%async_computation.4 | async-start | bytes 524288 | tf_op jit(solution)/shard_map/all_to_all | solution.py:389
  109.4 0.0 collective-permute-done.1.came
  109.4 0.1 shard_map.108.a
  109.4 2.2 %collective-permute-start.2 = (bf16[32,128]{1,0:T(8,128)(2,1)S(1)}, bf16[32,128]{1,0:T(8,128)(2,1)S(1)}, u32[]{:S(2)}, u32[]{:S(2)}) collective-permute-start(bf16[32,128]{1,0:T(8,128)(2,1)S(1)} %shard_map.108.a), channel_id=1, source_target_pairs={{0,256},{256,0},{512,768},{768,512},{1,257},{257,1},{513,769},{769... | collective-permute-start | bytes 24584 | tf_op jit(solution)/shard_map/ppermute | solution.py:392
  111.6 6.8 %collective-permute-done.2.b = bf16[32,128]{1,0:T(8,128)(2,1)S(1)} collective-permute-done((bf16[32,128]{1,0:T(8,128)(2,1)S(1)}, bf16[32,128]{1,0:T(8,128)(2,1)S(1)}, u32[]{:S(2)}, u32[]{:S(2)}) %collective-permute-start.2) | collective-permute-done | bytes 8224 | tf_op jit(solution)/shard_map/ppermute | solution.py:392
  118.4 0.1 shard_map.109.pair
  118.5 3.7 %collective-permute-start.3 = (bf16[32,128]{1,0:T(8,128)(2,1)S(1)}, bf16[32,128]{1,0:T(8,128)(2,1)S(1)}, u32[]{:S(2)}, u32[]{:S(2)}) collective-permute-start(bf16[32,128]{1,0:T(8,128)(2,1)S(1)} %shard_map.109.pair), channel_id=1, source_target_pairs={{0,512},{512,0},{256,768},{768,256},{1,513},{513,1},{257,769},{769... | collective-permute-start | bytes 24584 | tf_op jit(solution)/shard_map/ppermute | solution.py:395
  122.2 0.0 copy-start.5
  122.2 1.9 %shard_map.111 = bf16[2,160,2048]{2,1,0:T(8,128)(2,1)} custom-call(bf16[192,2560]{1,0:T(8,128)(2,1)S(1)} %get-tuple-element.26.mine, bf16[192,2560]{1,0:T(8,128)(2,1)S(1)} %collective-permute-done.1.came, bf16[160,160]{1,0:T(8,128)(2,1)S(1)} %get-tuple-element.28.gg, bf16[160,160]{1,0:T(8,128)(2,1)S(1)} %get-tuple-element.29.ug), custom_call_target="tpu_custom_call" | custom-call | flops 524288000 | tf_op jit(solution)/shard_map/pallas_call | solution.py:314
  124.1 0.1 collective-permute-done.3.far
  124.2 8.3 %all-to-all-done.4.ret = bf16[128,8,128]{2,1,0:T(8,128)(2,1)S(1)} async-done(((bf16[128,8,128]{2,1,0:T(8,128)(2,1)}), bf16[128,8,128]{2,1,0:T(8,128)(2,1)S(1)}, u32[]{:S(2)}, u32[]{:S(2)}) %all-to-all-start.4) | async-done | bytes 262176 | tf_op jit(solution)/shard_map/all_to_all | solution.py:389
  132.5 1.1 shard_map.110
  (7 shorter events, 0.1 us)
Async XLA Ops:
  2.5 18.9 %copy-start.6 = (bf16[32,16,128]{2,1,0:T(8,128)(2,1)S(1)}, bf16[32,16,128]{2,1,0:T(8,128)(2,1)}, u32[]{:S(2)}) copy-start(bf16[32,16,128]{2,1,0:T(8,128)(2,1)} %get-tuple-element.17) | copy-start | bytes 393220
  2.5 40.1 %copy-start.4 = (bf16[8,128]{1,0:T(8,128)(2,1)S(1)}, bf16[8,128]{1,0:T(8,128)(2,1)}, u32[]{:S(2)}) copy-start(bf16[8,128]{1,0:T(8,128)(2,1)} %get-tuple-element.18.tile_h.tile) | copy-start | bytes 6148
  5.4 37.2 %collective-permute-start = (bf16[496,2048]{1,0:T(8,128)(2,1)}, bf16[496,2048]{1,0:T(8,128)(2,1)S(1)}, u32[]{:S(2)}, u32[]{:S(2)}) collective-permute-start(bf16[496,2048]{1,0:T(8,128)(2,1)} %shard_map.104.mine), channel_id=1, source_target_pairs={{0,32},{32,0},{1,33},{33,1},{2,34},{34,2},{3,35},{35,3},{4,36},{36... | collective-permute-start | bytes 6094856 | tf_op jit(solution)/shard_map/ppermute | solution.py:370
  58.1 18.6 %copy-start = (bf16[496,2048]{1,0:T(8,128)(2,1)S(1)}, bf16[496,2048]{1,0:T(8,128)(2,1)}, u32[]{:S(2)}) copy-start(bf16[496,2048]{1,0:T(8,128)(2,1)} %shard_map.104.mine) | copy-start | bytes 6094852
  58.1 18.6 %copy-start.1 = (bf16[256,64]{0,1:T(8,128)(2,1)S(1)}, bf16[256,64]{0,1:T(8,128)(2,1)}, u32[]{:S(2)}) copy-start(bf16[256,64]{0,1:T(8,128)(2,1)} %param.8) | copy-start | bytes 98308
  58.1 18.6 %copy-start.2 = (f32[256,32]{0,1:T(8,128)S(1)}, f32[256,32]{0,1:T(8,128)}, u32[]{:S(2)}) copy-start(f32[256,32]{0,1:T(8,128)} %param.11) | copy-start | bytes 98308
  58.1 18.6 %copy-start.3 = (s32[256,1]{0,1:T(1,128)S(1)}, s32[256,1]{0,1:T(1,128)}, u32[]{:S(2)}) copy-start(s32[256,1]{0,1:T(1,128)} %param.12) | copy-start | bytes 3076
  90.6 18.8 %collective-permute-start.1 = (bf16[192,2560]{1,0:T(8,128)(2,1)S(1)}, bf16[192,2560]{1,0:T(8,128)(2,1)S(1)}, u32[]{:S(2)}, u32[]{:S(2)}) collective-permute-start(bf16[192,2560]{1,0:T(8,128)(2,1)S(1)} %get-tuple-element.26.mine), channel_id=1, source_target_pairs={{0,32},{32,0},{1,33},{33,1},{2,34},{34,2},{3,35},{35,3},{4,36},{36... | collective-permute-start | bytes 2949128 | tf_op jit(solution)/shard_map/ppermute | solution.py:390
  97.5 35.0 %all-to-all-start.4 = ((bf16[128,8,128]{2,1,0:T(8,128)(2,1)}), bf16[128,8,128]{2,1,0:T(8,128)(2,1)S(1)}, u32[]{:S(2)}, u32[]{:S(2)}) async-start(bf16[128,8,128]{2,1,0:T(8,128)(2,1)} %get-tuple-element.23), calls=%async_computation.4 | async-start | bytes 524288 | tf_op jit(solution)/shard_map/all_to_all | solution.py:389
  109.4 9.0 %collective-permute-start.2 = (bf16[32,128]{1,0:T(8,128)(2,1)S(1)}, bf16[32,128]{1,0:T(8,128)(2,1)S(1)}, u32[]{:S(2)}, u32[]{:S(2)}) collective-permute-start(bf16[32,128]{1,0:T(8,128)(2,1)S(1)} %shard_map.108.a), channel_id=1, source_target_pairs={{0,256},{256,0},{512,768},{768,512},{1,257},{257,1},{513,769},{769... | collective-permute-start | bytes 24584 | tf_op jit(solution)/shard_map/ppermute | solution.py:392
  118.5 5.7 %collective-permute-start.3 = (bf16[32,128]{1,0:T(8,128)(2,1)S(1)}, bf16[32,128]{1,0:T(8,128)(2,1)S(1)}, u32[]{:S(2)}, u32[]{:S(2)}) collective-permute-start(bf16[32,128]{1,0:T(8,128)(2,1)S(1)} %shard_map.109.pair), channel_id=1, source_target_pairs={{0,512},{512,0},{256,768},{768,256},{1,513},{513,1},{257,769},{769... | collective-permute-start | bytes 24584 | tf_op jit(solution)/shard_map/ppermute | solution.py:395
  122.2 10.3 %copy-start.5 = (bf16[64,32]{0,1:T(8,128)(2,1)S(1)}, bf16[64,32]{0,1:T(8,128)(2,1)}, u32[]{:S(2)}) copy-start(bf16[64,32]{0,1:T(8,128)(2,1)} %param.15) | copy-start | bytes 12292
